TPU v7x, 32 devices: a whole 2x2x4 slice. The times are simulated.
32 devices in a mesh: dp: 2 (over x), y: 4 (over z), x: 4 (over y, core).
Axes of the slice: x: 2, y: 2, z: 4, core: 2. Of those that a mesh axis runs over, the one named last changes fastest.
Arguments:
- tokens: int32 [3, 128], P(None, 'dp'), parts along dimension 1
- lengths: int32 [128], P('dp'), parts along dimension 0
- choices: int32 [3, 128, 2], P(None, 'dp'), parts along dimension 1
- emb_table: bfloat16 [122753, 2304], P(None, 'x')
- k_cache: bfloat16 [128, 128, 36, 64], P('dp', None, 'y'), parts along dimension 0
- v_cache: bfloat16 [128, 128, 36, 64], P('dp', None, 'y'), parts along dimension 0
- g_attn: bfloat16 [2304], P('x')
- w_q: bfloat16 [2304, 2304], P('x', 'y')
- w_k: bfloat16 [2304, 2304], P('x', 'y')
- w_v: bfloat16 [2304, 2304], P('x', 'y')
- w_o: bfloat16 [2304, 2304], P('y', 'x')
- g_ffn: bfloat16 [2304], P('x')
- w_router: bfloat16 [2304, 8], P('x')
- w_act: bfloat16 [8, 2304, 5760], P(None, 'x', 'y')
- w_lin: bfloat16 [8, 2304, 5760], P(None, 'x', 'y')
- w_down: bfloat16 [8, 5760, 2304], P(None, 'y', 'x')
Outputs:
- output 1: bfloat16 [3, 128, 2304], P(None, 'dp', 'x'), parts along dimension 1
- output 2: bfloat16 [128, 128, 36, 64], P('dp', None, 'y'), parts along dimension 0
- output 3: bfloat16 [128, 128, 36, 64], P('dp', None, 'y'), parts along dimension 0
There are 2 independent parts. A program takes and returns all parts, laid end to end along the dimension named above; an argument that names none is the same for every part.
All inputs are finite; a program needn't handle non-finite values.
Results may differ from a plain program's by a relative error of at most 0.0130543.
Values are sent between devices in bfloat16 or wider.
A program may use at most 1 GiB of HBM per device.

v0:
```python
import jax
import jax.numpy as jnp
from jax import lax
from jax.sharding import PartitionSpec as P

EPS = 1e-5
ROPE_BASE = 1.0e6


def shard_norm(x_val, gain_vec, width_full):
    x_f32 = x_val.astype(jnp.float32)
    sq_total = lax.psum(jnp.sum(x_f32 * x_f32, axis=-1, keepdims=True), 'x')
    return (x_f32 * lax.rsqrt(sq_total / width_full + EPS) * gain_vec.astype(jnp.float32)).astype(jnp.bfloat16)


def rotate(vectors, positions):
    head_dim = vectors.shape[-1]
    half_dim = head_dim // 2
    inv_freq = ROPE_BASE ** (-(jnp.arange(half_dim, dtype=jnp.float32) * 2.0 / head_dim))
    angle_shape = (vectors.shape[0],) + (1,) * (vectors.ndim - 2) + (half_dim,)
    angles = (positions.astype(jnp.float32)[:, None] * inv_freq[None, :]).reshape(angle_shape)
    cosine = jnp.cos(angles)
    sine_val = jnp.sin(angles)
    first_half = vectors[..., :half_dim].astype(jnp.float32)
    second_half = vectors[..., half_dim:].astype(jnp.float32)
    return jnp.concatenate([first_half * cosine - second_half * sine_val, second_half * cosine + first_half * sine_val], axis=-1).astype(jnp.bfloat16)


def write_slot(cache_arr, new_rows, positions):
    hit_mask = (jnp.arange(cache_arr.shape[1])[None, :] == positions[:, None])[:, :, None, None]
    return jnp.where(hit_mask, new_rows[:, None], cache_arr)


def attention(queries, key_cache, val_cache, positions):
    head_dim = queries.shape[-1]
    scores = jnp.einsum('bkgh,bskh->bkgs', queries, key_cache, preferred_element_type=jnp.float32) * head_dim ** -0.5
    valid_mask = (jnp.arange(key_cache.shape[1])[None, :] <= positions[:, None])[:, None, None, :]
    scores = jnp.where(valid_mask, scores, -1.0e30)
    peak_val = jnp.max(scores, axis=-1, keepdims=True)
    weight = jnp.where(valid_mask, jnp.exp(scores - peak_val), 0.0)
    total_w = jnp.sum(weight, axis=-1, keepdims=True)
    mixed_out = jnp.einsum('bkgs,bskh->bkgh', weight.astype(jnp.bfloat16), val_cache, preferred_element_type=jnp.float32)
    return (mixed_out / total_w).astype(jnp.bfloat16)


def mixing(logits, choice_row, experts):
    gate_val = jax.nn.softmax(jnp.take_along_axis(logits, choice_row, axis=1), axis=-1)
    onehot = choice_row[:, :, None] == jnp.arange(experts)[None, None, :]
    return jnp.sum(jnp.where(onehot, gate_val[:, :, None], 0.0), axis=1)


def solution(mesh):
    x_count = mesh.shape['x']
    cache_spec = P('dp', None, 'y', None)
    in_specs = (P(None, 'dp'), P('dp'), P(None, 'dp', None), P(None, 'x'), cache_spec, cache_spec, P('x'), P('x', 'y'), P('x', 'y'), P('x', 'y'), P('y', 'x'), P('x'), P('x', None), P(None, 'x', 'y'), P(None, 'x', 'y'), P(None, 'y', 'x'))
    out_specs = (P(None, 'dp', 'x'), cache_spec, cache_spec)

    def per_device(tokens, lengths, choices, emb_table, k_cache, v_cache, g_attn, w_q, w_k, w_v, w_o, g_ffn, w_router, w_act, w_lin, w_down):
        n_batch = tokens.shape[1]
        kv_local, head_dim = k_cache.shape[2], k_cache.shape[3]
        q_cols = w_q.shape[1]
        kv_cols = w_k.shape[1]
        group_size = q_cols // head_dim // kv_local
        width_full = emb_table.shape[1] * x_count
        experts = w_act.shape[0]
        key_cache, val_cache = k_cache, v_cache
        step_outs = []
        for step_idx in range(tokens.shape[0]):
            positions = lengths + step_idx
            x_in = jnp.take(emb_table, tokens[step_idx], axis=0)
            normed = shard_norm(x_in, g_attn, width_full)
            proj_part = jnp.concatenate([jnp.dot(normed, w_q, preferred_element_type=jnp.float32), jnp.dot(normed, w_k, preferred_element_type=jnp.float32), jnp.dot(normed, w_v, preferred_element_type=jnp.float32)], axis=1).astype(jnp.bfloat16)
            proj_sum = lax.psum(proj_part, 'x')
            queries = rotate(proj_sum[:, :q_cols].reshape(n_batch, kv_local, group_size, head_dim), positions)
            new_keys = rotate(proj_sum[:, q_cols:q_cols + kv_cols].reshape(n_batch, kv_local, head_dim), positions)
            new_vals = proj_sum[:, q_cols + kv_cols:].reshape(n_batch, kv_local, head_dim)
            key_cache = write_slot(key_cache, new_keys, positions)
            val_cache = write_slot(val_cache, new_vals, positions)
            mixed = attention(queries, key_cache, val_cache, positions).reshape(n_batch, q_cols)
            attn_sum = lax.psum(jnp.dot(mixed, w_o, preferred_element_type=jnp.float32).astype(jnp.bfloat16), 'y')
            x_mid = (x_in.astype(jnp.float32) + attn_sum.astype(jnp.float32)).astype(jnp.bfloat16)
            normed2 = shard_norm(x_mid, g_ffn, width_full)
            logits = lax.psum(jnp.dot(normed2, w_router, preferred_element_type=jnp.float32), 'x')
            coef = mixing(logits, choices[step_idx], experts)
            hidden_part = jnp.stack([jnp.einsum('bd,edf->ebf', normed2, w_act, preferred_element_type=jnp.float32), jnp.einsum('bd,edf->ebf', normed2, w_lin, preferred_element_type=jnp.float32)]).astype(jnp.bfloat16)
            hidden_sum = lax.psum(hidden_part, 'x')
            unit_bf16 = (coef.T[:, :, None] * jax.nn.silu(hidden_sum[0].astype(jnp.float32)) * hidden_sum[1].astype(jnp.float32)).astype(jnp.bfloat16)
            moe_sum = lax.psum(jnp.einsum('ebf,efd->bd', unit_bf16, w_down, preferred_element_type=jnp.float32).astype(jnp.bfloat16), 'y')
            step_outs.append((x_mid.astype(jnp.float32) + moe_sum.astype(jnp.float32)).astype(jnp.bfloat16))
        return jnp.stack(step_outs), key_cache, val_cache

    return jax.shard_map(per_device, mesh=mesh, in_specs=in_specs, out_specs=out_specs, check_vma=False)
```

profile of v0, /device:TPU:0, one launch (start us, length us, event | category | flops | bytes accessed | tf_op | source)
XLA Modules:
  0.0 662.6 jit_solution(9645885610742383603)
XLA Ops:
  8.1 173.6 %copy.64 = bf16[122753,576]{1,0:T(8,128)(2,1)} copy(bf16[122753,576]{0,1:T(8,128)(2,1)} %param.23) | data formatting | bytes 282822912 | tf_op args[3]
  187.2 8.4 %all-reduce.2 = (f32[64,1]{0,1:T(1,128)S(1)}, f32[64,1]{0,1:T(1,128)S(1)}, f32[64,1]{0,1:T(1,128)S(1)}) all-reduce(f32[64,1]{0,1:T(1,128)S(1)} %bitcast.305, f32[64,1]{0,1:T(1,128)S(1)} %bitcast.304, f32[64,1]{0,1:T(1,128)S(1)} %bitcast.303), channel_id=1, replica_groups=mesh['dp'=2,'y'=4,'x'=4] {'x'}, use_global_device_ids=true, to_apply=%region_29.32 | all-reduce | flops 192 | bytes 1536 | tf_op jit(solution)/shard_map/psum | solution.py:12
  201.8 33.9 %all-reduce.14.cloned.1.call-done = (bf16[64,1728]{1,0:T(8,128)(2,1)}, bf16[64,1728]{1,0:T(8,128)(2,1)}, bf16[64,1728]{1,0:T(8,128)(2,1)}) async-done(((bf16[64,1728]{1,0:T(8,128)(2,1)}, bf16[64,1728]{1,0:T(8,128)(2,1)}, bf16[64,1728]{1,0:T(8,128)(2,1)}), (bf16[64,1728]{1,0:T(8,128)(2,1)}, bf16[64,1728]{1,0:T(8,128)(2,1)}, bf16[64,1728]{1,0:T(8,128)(2,1)})) %all-reduce.14.cloned.1.call-update) | async-done | bytes 663568 | tf_op jit(solution)/shard_map/psum | solution.py:73
  239.0 8.4 %fusion.3 = f32[64,9,1,128]{3,2,1,0:T(1,128)S(1)} fusion(bf16[64,9,64,1]{2,3,1,0:T(2,128)(2,1)S(1)} %copy.88, bf16[64,128,9,64]{1,3,2,0:T(8,128)(2,1)} %param.24, pred[64,128]{1,0:T(8,128)(4,1)S(1)} %get-tuple-element.94, bf16[64,9,64]{2,1,0:T(8,128)(2,1)S(1)} %copy.67), kind=kOutput, calls=%fused_computation.15 | convolution fusion | flops 14155776 | bytes 9887744 | tf_op jit(solution)/shard_map/bkgh,bskh->bkgs/dot_general | solution.py:36
  248.2 8.5 %fusion.4 = f32[64,9,1,64]{3,2,1,0:T(1,128)S(1)} fusion(bf16[64,128,9,64]{1,3,2,0:T(8,128)(2,1)} %param.25, pred[64,128]{1,0:T(8,128)(4,1)S(1)} %get-tuple-element.94, bf16[64,9,64]{2,1,0:T(8,128)(2,1)S(1)} %copy.69, bf16[64,9,128,1]{2,0,1,3:T(8,128)(2,1)S(1)} %get-tuple-element.45), kind=kOutput, calls=%fused_computation.16 | convolution fusion | flops 14155776 | bytes 9814016 | tf_op jit(solution)/shard_map/bkgs,bskh->bkgh/dot_general | solution.py:42
  257.9 12.5 %fusion.5 = f32[64,9,1,128]{3,2,1,0:T(1,128)S(1)} fusion(bf16[64,9,64,1]{2,3,1,0:T(2,128)(2,1)S(1)} %copy.92, pred[64,128]{1,0:T(8,128)(4,1)S(1)} %get-tuple-element.108, bf16[64,128,9,64]{1,3,2,0:T(8,128)(2,1)} %param.24, pred[64,128]{1,0:T(8,128)(4,1)S(1)} %get-tuple-element.94, bf16[64,9,64]{2,1,0:T(8,128)(2,1)S(1)} %copy.75, ...), kind=kOutput, calls=%fused_computation.17 | convolution fusion | flops 18874368 | bytes 9969664 | tf_op jit(solution)/shard_map/bkgh,bskh->bkgs/dot_general | solution.py:36
  271.1 12.5 %fusion.6 = f32[64,9,1,64]{3,2,1,0:T(1,128)S(1)} fusion(pred[64,128]{1,0:T(8,128)(4,1)S(1)} %get-tuple-element.108, bf16[64,128,9,64]{1,3,2,0:T(8,128)(2,1)} %param.25, pred[64,128]{1,0:T(8,128)(4,1)S(1)} %get-tuple-element.94, bf16[64,9,64]{2,1,0:T(8,128)(2,1)S(1)} %copy.77, bf16[64,9,64]{2,1,0:T(8,128)(2,1)S(1)} %copy.69, ...), kind=kOutput, calls=%fused_computation.18 | convolution fusion | flops 18874368 | bytes 9895936 | tf_op jit(solution)/shard_map/bkgs,bskh->bkgh/dot_general | solution.py:42
  286.9 33.6 %broadcast_select_fusion.1 = (bf16[64,128,9,64]{1,3,2,0:T(8,128)(2,1)S(1)}, bf16[64,128,9,64]{1,3,2,0:T(8,128)(2,1)S(1)}) fusion(pred[64,128]{1,0:T(8,128)(4,1)S(1)} %get-tuple-element.98, bf16[64,128,9,64]{1,3,2,0:T(8,128)(2,1)} %param.24, pred[64,128]{1,0:T(8,128)(4,1)S(1)} %get-tuple-element.94, pred[64,128]{1,0:T(8,128)(4,1)S(1)} %get-tuple-element.108, ...), kind=kLoop, calls=%fused_computation.10 | loop fusion | flops 28311552 | bytes 38215680 | tf_op jit(solution)/shard_map/jit(_where)/select_n | solution.py:31
  324.6 2.8 copy-done.3
  327.3 5.0 fusion.82
  333.5 35.7 %all-reduce.18.cloned.1.call-done = (bf16[64,576]{1,0:T(8,128)(2,1)}, bf16[64,576]{1,0:T(8,128)(2,1)}, bf16[64,576]{1,0:T(8,128)(2,1)}) async-done(((bf16[64,576]{1,0:T(8,128)(2,1)}, bf16[64,576]{1,0:T(8,128)(2,1)}, bf16[64,576]{1,0:T(8,128)(2,1)}), (bf16[64,576]{1,0:T(8,128)(2,1)}, bf16[64,576]{1,0:T(8,128)(2,1)}, bf16[64,576]{1,0:T(8,128)(2,1)})) %all-reduce.18.cloned.1.call-update) | async-done | bytes 221200 | tf_op jit(solution)/shard_map/psum | solution.py:80
  372.5 5.8 all-reduce.1
  378.4 8.0 %fusion.31 = bf16[1,8,64,1440]{3,2,1,0:T(8,128)(2,1)S(1)} fusion(bf16[8,576,1440]{2,1,0:T(8,128)(2,1)} %param.33, bf16[64,576]{1,0:T(8,128)(2,1)S(1)} %get-tuple-element.33, f32[576]{0:T(1024)S(1)} %convert_element_type.270, f32[64]{0:T(128)S(1)} %rsqrt_bitcast_fusion.4), kind=kOutput, calls=%fused_computation.58 | convolution fusion | flops 850231296 | bytes 14821888 | tf_op jit(solution)/shard_map/bd,edf->ebf/dot_general | solution.py:85
  386.4 8.0 %fusion.32 = bf16[1,8,64,1440]{3,2,1,0:T(8,128)(2,1)S(1)} fusion(bf16[8,576,1440]{2,1,0:T(8,128)(2,1)} %param.34, bf16[64,576]{1,0:T(8,128)(2,1)S(1)} %get-tuple-element.33, f32[576]{0:T(1024)S(1)} %convert_element_type.270, f32[64]{0:T(128)S(1)} %rsqrt_bitcast_fusion.4), kind=kOutput, calls=%fused_computation.59 | convolution fusion | flops 850231296 | bytes 14821888 | tf_op jit(solution)/shard_map/bd,edf->ebf/dot_general | solution.py:85
  394.5 3.9 fusion.33
  398.4 4.0 fusion.34
  402.4 3.9 fusion.35
  406.2 2.8 fusion.36
  418.0 11.9 %all-reduce = (f32[64,8]{0,1:T(8,128)S(1)}, f32[64,8]{0,1:T(8,128)S(1)}, f32[64,8]{0,1:T(8,128)S(1)}) all-reduce(f32[64,8]{0,1:T(8,128)S(1)} %fusion.183, f32[64,8]{0,1:T(8,128)S(1)} %fusion.187, f32[64,8]{0,1:T(8,128)S(1)} %fusion.191), channel_id=1, replica_groups=mesh['dp'=2,'y'=4,'x'=4] {'x'}, use_global_device_ids=true, to_apply=%region_36.39 | all-reduce | flops 1536 | bytes 12288 | tf_op jit(solution)/shard_map/psum | solution.py:83
  433.9 152.4 %all-reduce.12.cloned.1.call-done = (bf16[2,8,64,1440]{3,2,1,0:T(8,128)(2,1)}, bf16[2,8,64,1440]{3,2,1,0:T(8,128)(2,1)}, bf16[2,8,64,1440]{3,2,1,0:T(8,128)(2,1)}) async-done(((bf16[2,8,64,1440]{3,2,1,0:T(8,128)(2,1)}, bf16[2,8,64,1440]{3,2,1,0:T(8,128)(2,1)}, bf16[2,8,64,1440]{3,2,1,0:T(8,128)(2,1)}), (bf16[2,8,64,1440]{3,2,1,0:T(8,128)(2,1)}, bf16[2,8,64,1440]{3,2,1,0:T(8,128)(2,1)}, ...) | async-done | bytes 8847376 | tf_op jit(solution)/shard_map/psum | solution.py:86
  586.3 10.9 %fusion.67 = bf16[64,576]{1,0:T(8,128)(2,1)} fusion(bf16[8,1440,576]{1,2,0:T(8,128)(2,1)} %param.35, bf16[2,8,64,1440]{3,2,1,0:T(8,128)(2,1)} %get-tuple-element.16, f32[8,64]{1,0:T(8,128)S(1)} %bitcast.297), kind=kOutput, calls=%fused_computation.91 | convolution fusion | flops 856018944 | bytes 16295936 | tf_op jit(solution)/shard_map/ebf,efd->bd/dot_general | solution.py:88
  597.2 11.0 %fusion.70 = bf16[64,576]{1,0:T(8,128)(2,1)} fusion(bf16[8,1440,576]{1,2,0:T(8,128)(2,1)} %param.35, bf16[2,8,64,1440]{3,2,1,0:T(8,128)(2,1)} %get-tuple-element.15, f32[8,64]{1,0:T(8,128)S(1)} %bitcast.298), kind=kOutput, calls=%fused_computation.92 | convolution fusion | flops 856018944 | bytes 16295936 | tf_op jit(solution)/shard_map/ebf,efd->bd/dot_general | solution.py:88
  608.2 8.2 %fusion.73 = bf16[64,576]{1,0:T(8,128)(2,1)} fusion(bf16[8,1440,576]{1,2,0:T(8,128)(2,1)} %param.35, bf16[2,8,64,1440]{3,2,1,0:T(8,128)(2,1)S(1)} %copy-done.15, f32[8,64]{1,0:T(8,128)S(1)} %bitcast.299), kind=kOutput, calls=%fused_computation.93 | convolution fusion | flops 856018944 | bytes 16295936 | tf_op jit(solution)/shard_map/ebf,efd->bd/dot_general | solution.py:88
  616.4 36.0 %all-reduce.16.cloned.1.call-done = (bf16[64,576]{1,0:T(8,128)(2,1)}, bf16[64,576]{1,0:T(8,128)(2,1)}, bf16[64,576]{1,0:T(8,128)(2,1)}) async-done(((bf16[64,576]{1,0:T(8,128)(2,1)}, bf16[64,576]{1,0:T(8,128)(2,1)}, bf16[64,576]{1,0:T(8,128)(2,1)}), (bf16[64,576]{1,0:T(8,128)(2,1)}, bf16[64,576]{1,0:T(8,128)(2,1)}, bf16[64,576]{1,0:T(8,128)(2,1)})) %all-reduce.16.cloned.1.call-update) | async-done | bytes 221200 | tf_op jit(solution)/shard_map/psum | solution.py:88
  (181 shorter events, 46.2 us)
Async XLA Ops:
  7.2 188.5 %copy-start = (bf16[576,576]{1,0:T(8,128)(2,1)S(1)}, bf16[576,576]{1,0:T(8,128)(2,1)}, u32[]{:S(2)}) copy-start(bf16[576,576]{1,0:T(8,128)(2,1)} %param.29) | copy-start | bytes 1990660
  7.2 228.6 %all-reduce.14.cloned.1.call-start = ((), (), s32[]{:S(2)}) async-start(), calls=%async_computation.1 | async-start | bytes 1376256 | tf_op jit(solution)/shard_map/psum | solution.py:73
  8.0 187.6 %copy-start.12 = (bf16[576]{0:T(1024)(128)(2,1)S(1)}, bf16[576]{0:T(1024)(128)(2,1)}, u32[]{:S(2)}) copy-start(bf16[576]{0:T(1024)(128)(2,1)} %param.26) | copy-start | bytes 3460
  8.1 187.9 %copy-start.4 = (bf16[576,576]{1,0:T(8,128)(2,1)S(1)}, bf16[576,576]{1,0:T(8,128)(2,1)}, u32[]{:S(2)}) copy-start(bf16[576,576]{1,0:T(8,128)(2,1)} %param.28) | copy-start | bytes 1990660
  181.7 15.2 %copy-start.5 = (bf16[576,576]{1,0:T(8,128)(2,1)S(1)}, bf16[576,576]{1,0:T(8,128)(2,1)}, u32[]{:S(2)}) copy-start(bf16[576,576]{1,0:T(8,128)(2,1)} %param.27) | copy-start | bytes 1990660
  196.0 5.4 copy-start.14
  201.0 168.2 %all-reduce.18.cloned.1.call-start = ((), (), s32[]{:S(2)}) async-start(), calls=%async_computation.3 | async-start | bytes 491520 | tf_op jit(solution)/shard_map/psum | solution.py:80
  248.2 8.8 %copy-start.10 = (bf16[64,1728]{1,0:T(8,128)(2,1)S(1)}, bf16[64,1728]{1,0:T(8,128)(2,1)}, u32[]{:S(2)}) copy-start(bf16[64,1728]{1,0:T(8,128)(2,1)} %get-tuple-element.17) | copy-start | bytes 663556
  271.1 12.8 %copy-start.6 = (bf16[576,576]{1,0:T(8,128)(2,1)S(1)}, bf16[576,576]{1,0:T(8,128)(2,1)}, u32[]{:S(2)}) copy-start(bf16[576,576]{1,0:T(8,128)(2,1)} %param.30) | copy-start | bytes 1990660
  320.5 3.7 copy-start.2
  320.5 6.8 %copy-start.3 = (bf16[64,128,9,64]{1,3,2,0:T(8,128)(2,1)}, bf16[64,128,9,64]{1,3,2,0:T(8,128)(2,1)S(1)}, u32[]{:S(2)}) copy-start(bf16[64,128,9,64]{1,3,2,0:T(8,128)(2,1)S(1)} %get-tuple-element.72) | copy-start | bytes 28311556
  327.3 6.2 copy-start.13
  333.5 252.8 %all-reduce.12.cloned.1.call-start = ((), (), s32[]{:S(2)}) async-start(), calls=%async_computation | async-start | bytes 18874368 | tf_op jit(solution)/shard_map/psum | solution.py:86
  378.4 16.0 %slice-start = ((s8[14155776]{0:T(1024)(128)(4,1)}), s8[4194304]{0:T(1024)(128)(4,1)S(1)}, s32[]{:S(2)}) async-start(s8[14155776]{0:T(1024)(128)(4,1)} %bitcast.281), calls=%async_computation.4 | async-start | bytes 8388608
  378.4 16.0 %slice-start.1 = ((s8[14155776]{0:T(1024)(128)(4,1)}), s8[4194304]{0:T(1024)(128)(4,1)S(1)}, s32[]{:S(2)}) async-start(s8[14155776]{0:T(1024)(128)(4,1)} %bitcast.281), calls=%async_computation.5 | async-start | bytes 8388608
  386.4 8.1 %slice-start.2 = ((s8[14155776]{0:T(1024)(128)(4,1)}), s8[4194304]{0:T(1024)(128)(4,1)S(1)}, s32[]{:S(2)}) async-start(s8[14155776]{0:T(1024)(128)(4,1)} %bitcast.281), calls=%async_computation.6 | async-start | bytes 8388608
  386.4 8.0 %slice-start.3 = ((s8[14155776]{0:T(1024)(128)(4,1)}), s8[1572864]{0:T(1024)(128)(4,1)S(1)}, s32[]{:S(2)}) async-start(s8[14155776]{0:T(1024)(128)(4,1)} %bitcast.281), calls=%async_computation.7 | async-start | bytes 3145728
  386.4 12.0 %slice-start.4 = ((s8[14155776]{0:T(1024)(128)(4,1)}), s8[4194304]{0:T(1024)(128)(4,1)S(1)}, s32[]{:S(2)}) async-start(s8[14155776]{0:T(1024)(128)(4,1)} %bitcast.283), calls=%async_computation.8 | async-start | bytes 8388608
  386.4 11.9 %slice-start.5 = ((s8[14155776]{0:T(1024)(128)(4,1)}), s8[4194304]{0:T(1024)(128)(4,1)S(1)}, s32[]{:S(2)}) async-start(s8[14155776]{0:T(1024)(128)(4,1)} %bitcast.283), calls=%async_computation.9 | async-start | bytes 8388608
  394.4 4.0 slice-start.6
  394.5 3.9 slice-start.7
  416.0 236.4 %all-reduce.16.cloned.1.call-start = ((), (), s32[]{:S(2)}) async-start(), calls=%async_computation.2 | async-start | bytes 491520 | tf_op jit(solution)/shard_map/psum | solution.py:88
  597.2 11.0 %copy-start.15 = (bf16[2,8,64,1440]{3,2,1,0:T(8,128)(2,1)S(1)}, bf16[2,8,64,1440]{3,2,1,0:T(8,128)(2,1)}, u32[]{:S(2)}) copy-start(bf16[2,8,64,1440]{3,2,1,0:T(8,128)(2,1)} %get-tuple-element.14) | copy-start | bytes 8847364
  608.2 47.7 %copy-start.1 = (bf16[576,576]{1,0:T(8,128)(2,1)S(1)}, bf16[576,576]{1,0:T(8,128)(2,1)}, u32[]{:S(2)}) copy-start(bf16[576,576]{1,0:T(8,128)(2,1)} %param.29) | copy-start | bytes 1990660
  (5 other events, 9.1 us)
Sparse Core Ops, SparseCore 0:
  201.1 34.5 all-reduce.13
  333.6 35.6 all-reduce.17
  416.1 170.1 all-reduce.11
  616.6 35.7 all-reduce.15
where the time goes:
time: 671 us; the launch traced here: 663 us
  waiting for transfers between devices  258 us (38%)
  local copies, waits for them, and re-layouts  197 us (29%)
  matrix products  116 us (17%)
  other arithmetic  49.8 us (7%)
  blocking collectives  26.2 us (4%)
  between operations  14.8 us (2%)
    unnamed x51, local copies, waits for them, and re-layouts  179 us
    psum x1, waiting for transfers between devices, per_device(): hidden_sum = lax.psum(hidden_part, 'x')  152 us
    psum x1, waiting for transfers between devices, per_device(): lax.psum(jnp.einsum('ebf,efd->bd', unit_bf16, w_down, preferred_element_t...  36 us
    psum x1, waiting for transfers between devices, per_device(): lax.psum(jnp.dot(mixed, w_o, preferred_element_type=jnp.float32).astype(j...  35.7 us
    psum x1, waiting for transfers between devices, per_device(): proj_sum = lax.psum(proj_part, 'x')  33.9 us
    select_n x1, other arithmetic, write_slot(): return jnp.where(hit_mask, new_rows[:, None], cache_arr)  33.6 us
    dot_general x3, matrix products, per_device(): jnp.einsum('ebf,efd->bd', unit_bf16, w_down, preferred_element_type=jnp.f...  30.1 us
    dot_general x3, matrix products, attention(): jnp.einsum('bkgs,bskh->bkgh', weight.astype(jnp.bfloat16), val_cache, pre...  26 us
  transfers between devices with their start and end apart: 4, of which 4 were waited for; matrix products, arithmetic and copies ran while one was open for 1% of the time, Pallas kernels for 0%

commit v1 on v0

v1 whole, which is shorter than its diff:
```python
import functools

import jax
import jax.numpy as jnp
from jax import lax
from jax.experimental import pallas as pl
from jax.experimental.pallas import tpu as pltpu
from jax.sharding import PartitionSpec as P

EPS = 1e-5
ROPE_BASE = 1.0e6
F32 = jnp.float32
BF16 = jnp.bfloat16


def dot(a, b):
    return lax.dot_general(a, b, (((1,), (0,)), ((), ())), preferred_element_type=F32)


def dot_nt(a, b):
    return lax.dot_general(a, b, (((1,), (1,)), ((), ())), preferred_element_type=F32)


def attention_kernel(steps, batch, block, heads, head, lens_ref, qkv_ref, cos_ref, sin_ref, swap_ref, k_in, v_in, o_ref, k_out, v_out, q_rows, kt_ref, vt_ref, o_rows):
    cols = heads * head
    slots = k_in.shape[-1]
    rows = steps * batch
    i = pl.program_id(0)
    hpad = 16

    @pl.when(i == 0)
    def _():
        cosine, sine = cos_ref[...], sin_ref[...]
        for part in range(2):
            val = qkv_ref[:, part * cols:(part + 1) * cols]
            swapped = dot(val, swap_ref[...])
            rot = (val.astype(F32) * cosine + swapped * sine).astype(BF16).astype(F32)
            if part == 0:
                q_rows[...] = rot.reshape(steps, batch, cols)
            else:
                kt_ref[...] = rot.T.astype(BF16)
        vt_ref[...] = qkv_ref[:, 2 * cols:].astype(F32).T.astype(BF16)

    pair = 2
    row_id = lax.broadcasted_iota(jnp.int32, (rows, pair * slots), 0)
    lane_id = lax.broadcasted_iota(jnp.int32, (rows, pair * slots), 1)
    row_t, row_b = row_id // batch, row_id % batch
    lane_s, lane_j = lane_id % slots, lane_id // slots
    head_mask = lax.broadcasted_iota(jnp.int32, (hpad, cols), 1) // head == lax.broadcasted_iota(jnp.int32, (hpad, cols), 0)
    t_of = lax.broadcasted_iota(jnp.int32, (steps * hpad, slots), 0) // hpad
    s_of = lax.broadcasted_iota(jnp.int32, (steps * hpad, slots), 1)
    slot_id = lax.broadcasted_iota(jnp.int32, (cols, slots), 1)

    for p in range(block // pair):
        b0 = i * block + p * pair
        len0, len1 = lens_ref[b0], lens_ref[b0 + 1]
        length = jnp.where(lane_j == 0, len0, len1)
        hot = jnp.where((row_b == b0 + lane_j) & (lane_s == length + row_t), 1.0, 0.0).astype(BF16)
        k_patch = dot(kt_ref[...], hot).astype(BF16)
        v_patch = dot(vt_ref[...], hot).astype(BF16)
        for j in range(pair):
            n = p * pair + j
            b = b0 + j
            first = len0 if j == 0 else len1
            fresh = (slot_id >= first) & (slot_id < first + steps)
            k_new = jnp.where(fresh, k_patch[:, j * slots:(j + 1) * slots], k_in[n].reshape(cols, slots))
            v_new = jnp.where(fresh, v_patch[:, j * slots:(j + 1) * slots], v_in[n].reshape(cols, slots))
            k_out[n] = k_new.reshape(heads, head, slots)
            v_out[n] = v_new.reshape(heads, head, slots)
            q_blk = jnp.concatenate([jnp.where(head_mask, jnp.broadcast_to(q_rows[t, pl.ds(b, 1), :], (hpad, cols)), 0.0) for t in range(steps)], axis=0).astype(BF16)
            scores = dot(q_blk, k_new) * head ** -0.5
            valid = s_of <= first + t_of
            scores = jnp.where(valid, scores, -1.0e30)
            peak = jnp.max(scores, axis=-1, keepdims=True)
            weight = jnp.where(valid, jnp.exp(scores - peak), 0.0)
            total = jnp.sum(weight, axis=-1, keepdims=True)
            mixed = dot_nt(weight.astype(BF16), v_new) / total
            for t in range(steps):
                o_rows[t, pl.ds(b, 1), :] = jnp.sum(jnp.where(head_mask, mixed[t * hpad:(t + 1) * hpad], 0.0), axis=0, keepdims=True)

    @pl.when(i == pl.num_programs(0) - 1)
    def _():
        o_ref[...] = o_rows[...].reshape(rows, cols).astype(BF16)


def attention(lengths, qkv, cos_t, sin_t, k_cache, v_cache, steps):
    batch, slots, heads, head = k_cache.shape
    cols, rows, block = heads * head, steps * batch, 4
    k_t, v_t = jnp.transpose(k_cache, (0, 2, 3, 1)), jnp.transpose(v_cache, (0, 2, 3, 1))
    src = jnp.arange(cols)[:, None]
    dst = jnp.arange(cols)[None, :]
    low = dst % head < head // 2
    swap = (jnp.where(low & (src == dst + head // 2), -1.0, 0.0) + jnp.where(~low & (src == dst - head // 2), 1.0, 0.0)).astype(BF16)
    whole = lambda shape: pl.BlockSpec(shape, lambda i: (0,) * len(shape))
    cache_blk = pl.BlockSpec((block, heads, head, slots), lambda i: (i, 0, 0, 0))
    o, k_o, v_o = pl.pallas_call(
        functools.partial(attention_kernel, steps, batch, block, heads, head),
        grid=(batch // block,),
        in_specs=[pl.BlockSpec(memory_space=pltpu.SMEM), whole((rows, 3 * cols)), whole((rows, cols)), whole((rows, cols)), whole((cols, cols)), cache_blk, cache_blk],
        out_specs=[whole((rows, cols)), cache_blk, cache_blk],
        out_shape=[jax.ShapeDtypeStruct((rows, cols), BF16), jax.ShapeDtypeStruct(k_t.shape, BF16), jax.ShapeDtypeStruct(v_t.shape, BF16)],
        scratch_shapes=[pltpu.VMEM((steps, batch, cols), F32), pltpu.VMEM((cols, rows), BF16), pltpu.VMEM((cols, rows), BF16), pltpu.VMEM((steps, batch, cols), F32)],
        compiler_params=pltpu.CompilerParams(dimension_semantics=("arbitrary",)),
        cost_estimate=pl.CostEstimate(flops=4 * 10 ** 9, bytes_accessed=4 * k_t.size * 2, transcendentals=0),
        name="attention",
    )(lengths, qkv, cos_t, sin_t, swap, k_t, v_t)
    back = lambda a: jnp.transpose(a, (0, 3, 1, 2))
    return o, back(k_o), back(v_o)


def rope_tables(lengths, steps, heads, head):
    half = head // 2
    inv_freq = ROPE_BASE ** (-(jnp.arange(half, dtype=F32) * 2.0 / head))
    positions = (lengths[None, :] + jnp.arange(steps)[:, None]).reshape(-1).astype(F32)
    angles = positions[:, None] * inv_freq[None, :]
    tile = lambda a: jnp.concatenate([a] * (2 * heads), axis=1)
    return tile(jnp.cos(angles)), tile(jnp.sin(angles))


def shard_norm(x_val, gain_vec, width_full):
    x_f32 = x_val.astype(F32)
    sq_total = lax.psum(jnp.sum(x_f32 * x_f32, axis=-1, keepdims=True), 'x')
    return (x_f32 * lax.rsqrt(sq_total / width_full + EPS) * gain_vec.astype(F32)).astype(BF16)


def solution(mesh):
    x_count = mesh.shape['x']
    cache_spec = P('dp', None, 'y', None)
    in_specs = (P(None, 'dp'), P('dp'), P(None, 'dp', None), P(None, 'x'), cache_spec, cache_spec, P('x'), P('x', 'y'), P('x', 'y'), P('x', 'y'), P('y', 'x'), P('x'), P('x', None), P(None, 'x', 'y'), P(None, 'x', 'y'), P(None, 'y', 'x'))
    out_specs = (P(None, 'dp', 'x'), cache_spec, cache_spec)

    def per_device(tokens, lengths, choices, emb_table, k_cache, v_cache, g_attn, w_q, w_k, w_v, w_o, g_ffn, w_router, w_act, w_lin, w_down):
        steps, n_batch = tokens.shape
        heads, head = k_cache.shape[2], k_cache.shape[3]
        rows = steps * n_batch
        width_full = emb_table.shape[1] * x_count
        experts, width, ff = w_act.shape
        cos_t, sin_t = rope_tables(lengths, steps, heads, head)
        x_in = jnp.take(emb_table, tokens.reshape(rows), axis=0)
        normed = shard_norm(x_in, g_attn, width_full)
        qkv_part = jnp.concatenate([dot(normed, w_q), dot(normed, w_k), dot(normed, w_v)], axis=1).astype(BF16)
        qkv = lax.psum(qkv_part, 'x')
        mixed, k_out, v_out = attention(lengths, qkv, cos_t, sin_t, k_cache, v_cache, steps)
        attn_sum = lax.psum(dot(mixed, w_o).astype(BF16), 'y')
        x_mid = (x_in.astype(F32) + attn_sum.astype(F32)).astype(BF16)
        normed2 = shard_norm(x_mid, g_ffn, width_full)
        logits = lax.psum(dot(normed2, w_router), 'x')
        choice = choices.reshape(rows, 2)
        hot = choice[:, :, None] == jnp.arange(experts)[None, None, :]
        picked = jnp.sum(jnp.where(hot, logits[:, None, :], 0.0), axis=-1)
        gate = jax.nn.softmax(picked, axis=-1)
        hot_t = jnp.transpose(hot, (1, 0, 2))
        sparse = jnp.where(hot_t[..., None], normed2[None, :, None, :], 0).reshape(2 * rows, experts * width)
        hid_part = jnp.stack([dot(sparse, w_act.reshape(experts * width, ff)), dot(sparse, w_lin.reshape(experts * width, ff))]).astype(BF16)
        hid = lax.psum(hid_part, 'x').astype(F32)
        unit = (gate.T.reshape(2 * rows, 1) * jax.nn.silu(hid[0]) * hid[1]).astype(BF16).reshape(2, rows, ff)
        unit_e = jnp.sum(jnp.where(jnp.transpose(hot_t, (2, 0, 1))[..., None], unit[None], 0), axis=1)
        moe = lax.psum(jnp.einsum('ebf,efd->bd', unit_e, w_down, preferred_element_type=F32).astype(BF16), 'y')
        out = (x_mid.astype(F32) + moe.astype(F32)).astype(BF16)
        return out.reshape(steps, n_batch, width), k_out, v_out

    return jax.shard_map(per_device, mesh=mesh, in_specs=in_specs, out_specs=out_specs, check_vma=False)
```

time: 671 us -> 475 us (0.71)
  waiting for transfers between devices: 258 us -> 147 us
  matrix products: 116 us -> 39.4 us
  other arithmetic: 49.8 us -> 15.5 us
  Pallas kernels: 0 us -> 32.6 us
    psum x4, waiting for transfers between devices: 258 us -> 147 us  [the longest x1 46.3 us: per_device(): hid = lax.psum(hid_part, 'x').astype(F32)]
    dot_general x30 -> x8, matrix products: 116 us -> 39.4 us  [the longest x7 27.1 us: dot(): lax.dot_general(a, b, (((1,), (0,)), ((), ())), preferred_element_type=F32)]
    pallas_call x0 -> x1, Pallas kernels: none -> 32.6 us  [attention(): pl.pallas_call(functools.partial(attention_kernel, steps, batch, block, h...]
    select_n x1 -> x2, other arithmetic: 33.6 us -> 2.31 us  [the longest x1 2.31 us: per_device(): jnp.where(hot_t[..., None], normed2[None, :, None, :], 0)]
    another operation x9 -> x1, other arithmetic: 9.5 us -> 1.6 us  [per_device(): jnp.stack([dot(sparse, w_act.reshape(experts * width, ff)), dot(sparse, w...]
    select_n x0 -> x1, local copies, waits for them, and re-layouts: none -> 7.19 us  [per_device(): jnp.where(hot_t[..., None], normed2[None, :, None, :], 0)]
    unnamed x51 -> x22, local copies, waits for them, and re-layouts: 179 us -> 174 us
where the time goes in v1:
time: 475 us; the launch traced here: 470 us
  local copies, waits for them, and re-layouts  200 us (42%)
  waiting for transfers between devices  147 us (31%)
  matrix products  39.4 us (8%)
  Pallas kernels  32.6 us (7%)
  blocking collectives  21.3 us (4%)
  other arithmetic  15.5 us (3%)
  between operations  14 us (3%)
    unnamed x22, local copies, waits for them, and re-layouts  174 us
    psum x1, waiting for transfers between devices, per_device(): hid = lax.psum(hid_part, 'x').astype(F32)  46.3 us
    psum x1, waiting for transfers between devices, per_device(): lax.psum(jnp.einsum('ebf,efd->bd', unit_e, w_down, preferred_element_type...  35.6 us
    psum x1, waiting for transfers between devices, per_device(): attn_sum = lax.psum(dot(mixed, w_o).astype(BF16), 'y')  35.5 us
    pallas_call x1, Pallas kernels, attention(): pl.pallas_call(functools.partial(attention_kernel, steps, batch, block, h...  32.6 us
    psum x1, waiting for transfers between devices, per_device(): qkv = lax.psum(qkv_part, 'x')  29.6 us
    dot_general x7, matrix products, dot(): lax.dot_general(a, b, (((1,), (0,)), ((), ())), preferred_element_type=F32)  27.1 us
    psum x2, blocking collectives, shard_norm(): sq_total = lax.psum(jnp.sum(x_f32 * x_f32, axis=-1, keepdims=True), 'x')  14.3 us
  transfers between devices with their start and end apart: 4, of which 4 were waited for; matrix products, arithmetic and copies ran while one was open for 1% of the time, Pallas kernels for 0%

profile of v1, /device:TPU:0, one launch (start us, length us, event | category | flops | bytes accessed | tf_op | source)
XLA Modules:
  0.0 470.0 jit_solution(11243864486583864019)
XLA Ops:
  8.8 173.6 %copy.30 = bf16[122753,576]{1,0:T(8,128)(2,1)} copy(bf16[122753,576]{0,1:T(8,128)(2,1)} %param.19) | data formatting | bytes 282822912 | tf_op args[3]
  182.4 4.7 gather_fusion
  187.3 8.4 %psum.49 = f32[192,1]{0,1:T(1,128)S(1)} all-reduce(f32[192,1]{0,1:T(1,128)S(1)} %bitcast.51), channel_id=1, replica_groups=mesh['dp'=2,'y'=4,'x'=4] {'x'}, use_global_device_ids=true, to_apply=%region_1.2 | all-reduce | flops 192 | bytes 1536 | tf_op jit(solution)/shard_map/psum | solution.py:122
  201.7 1.5 add_convert_fusion.swap_ref
  203.2 29.6 %all-reduce.5.cloned.1.call-done.qkv_ref = bf16[192,1728]{1,0:T(8,128)(2,1)} async-done(((bf16[192,1728]{1,0:T(8,128)(2,1)}), bf16[192,1728]{1,0:T(8,128)(2,1)}) %all-reduce.5.cloned.1.call-update) | async-done | bytes 663568 | tf_op jit(solution)/shard_map/psum | solution.py:142
  232.8 32.6 %attention.1 = (bf16[192,576]{1,0:T(8,128)(2,1)}, bf16[64,9,64,128]{3,2,1,0:T(8,128)(2,1)}, bf16[64,9,64,128]{3,2,1,0:T(8,128)(2,1)}) custom-call(s32[64]{0:T(128)} %lens_ref.1, bf16[192,1728]{1,0:T(8,128)(2,1)} %all-reduce.5.cloned.1.call-done.qkv_ref, f32[192,576]{1,0:T(8,128)} %concatenate.11.cos_ref, f32[192,576]{1,0:T(8,128)} %concatenate.12.sin_ref, ...), custom_call_target="tpu_custom_call" | custom-call | flops 4000000000 | bytes 37748736 | tf_op jit(solution)/shard_map/attention/pallas_call | solution.py:96
  265.4 2.0 convolution_convert_fusion.2
  267.6 35.5 %all-reduce.7.cloned.1.call-done = bf16[192,576]{1,0:T(8,128)(2,1)} async-done(((bf16[192,576]{1,0:T(8,128)(2,1)}), bf16[192,576]{1,0:T(8,128)(2,1)}) %all-reduce.7.cloned.1.call-update) | async-done | bytes 221200 | tf_op jit(solution)/shard_map/psum | solution.py:144
  304.3 5.8 %psum.52 = f32[192,1]{0,1:T(1,128)S(1)} all-reduce(f32[192,1]{0,1:T(1,128)S(1)} %bitcast.49), channel_id=1, replica_groups=mesh['dp'=2,'y'=4,'x'=4] {'x'}, use_global_device_ids=true, to_apply=%region_5.6 | all-reduce | flops 192 | bytes 1536 | tf_op jit(solution)/shard_map/psum | solution.py:122
  310.3 2.3 broadcast_select_fusion
  312.6 7.2 %select_n.76 = bf16[384,4608]{1,0:T(8,128)(2,1)} reshape(bf16[2,192,8,576]{3,2,1,0:T(8,128)(2,1)} %broadcast_select_fusion) | data formatting | bytes 7077888 | tf_op jit(solution)/shard_map/jit(_where)/select_n | solution.py:153
  319.8 13.7 %fusion = bf16[1,384,1440]{1,2,0:T(8,128)(2,1)S(1)} fusion(bf16[384,4608]{1,0:T(8,128)(2,1)} %select_n.76, bf16[4608,1440]{1,0:T(8,128)(2,1)} %bitcast.56), kind=kOutput, calls=%fused_computation.5 | convolution fusion | flops 5096632320 | bytes 17915904 | tf_op jit(solution)/shard_map/dot_general | solution.py:17
  333.4 10.0 %fusion.1 = bf16[1,384,1440]{1,2,0:T(8,128)(2,1)S(1)} fusion(bf16[384,4608]{1,0:T(8,128)(2,1)S(1)} %copy-done.1, bf16[4608,1440]{1,0:T(8,128)(2,1)} %bitcast.57), kind=kOutput, calls=%fused_computation.6 | convolution fusion | flops 5096632320 | bytes 17915904 | tf_op jit(solution)/shard_map/dot_general | solution.py:17
  343.5 1.6 pad_maximum_fusion
  345.3 7.0 %psum.53 = f32[192,8]{0,1:T(8,128)S(1)} all-reduce(f32[192,8]{0,1:T(8,128)S(1)} %fusion.24), channel_id=1, replica_groups=mesh['dp'=2,'y'=4,'x'=4] {'x'}, use_global_device_ids=true, to_apply=%region_6.7 | all-reduce | flops 1536 | bytes 12288 | tf_op jit(solution)/shard_map/psum | solution.py:147
  352.4 46.3 %all-reduce.9.cloned.1.call-done = bf16[2,384,1440]{1,2,0:T(8,128)(2,1)} async-done(((bf16[2,384,1440]{1,2,0:T(8,128)(2,1)}), bf16[2,384,1440]{1,2,0:T(8,128)(2,1)}) %all-reduce.9.cloned.1.call-update) | async-done | bytes 2211856 | tf_op jit(solution)/shard_map/psum | solution.py:155
  398.7 3.9 fusion.23
  402.6 2.0 copy.32
  404.6 3.1 copy.33
  407.8 2.3 multiply_convert_fusion
  410.1 3.8 select_reduce_fusion
  413.9 12.3 %fusion.4 = bf16[192,576]{1,0:T(8,128)(2,1)} fusion(bf16[8,192,1440]{2,1,0:T(8,128)(2,1)} %select_reduce_fusion, bf16[8,1440,576]{1,2,0:T(8,128)(2,1)} %param.31), kind=kOutput, calls=%fused_computation.19 | convolution fusion | flops 2548150272 | bytes 17915904 | tf_op jit(solution)/shard_map/ebf,efd->bd/dot_general | solution.py:158
  426.2 35.6 %all-reduce.11.cloned.1.call-done = bf16[192,576]{1,0:T(8,128)(2,1)} async-done(((bf16[192,576]{1,0:T(8,128)(2,1)}), bf16[192,576]{1,0:T(8,128)(2,1)}) %all-reduce.11.cloned.1.call-update) | async-done | bytes 221200 | tf_op jit(solution)/shard_map/psum | solution.py:158
  461.7 1.7 fusion.12
  (61 shorter events, 9.5 us)
Async XLA Ops:
  7.2 188.6 %copy-start = (bf16[576,576]{1,0:T(8,128)(2,1)S(1)}, bf16[576,576]{1,0:T(8,128)(2,1)}, u32[]{:S(2)}) copy-start(bf16[576,576]{1,0:T(8,128)(2,1)} %param.25) | copy-start | bytes 1990660
  7.2 225.6 %all-reduce.5.cloned.1.call-start = ((), (), s32[]{:S(2)}) async-start(), calls=%async_computation | async-start | bytes 1376256 | tf_op jit(solution)/shard_map/psum | solution.py:142
  182.4 13.4 %copy-start.6 = (bf16[576]{0:T(1024)(128)(2,1)S(1)}, bf16[576]{0:T(1024)(128)(2,1)}, u32[]{:S(2)}) copy-start(bf16[576]{0:T(1024)(128)(2,1)} %param.22) | copy-start | bytes 3460
  182.4 13.9 %copy-start.8 = (bf16[576,576]{1,0:T(8,128)(2,1)S(1)}, bf16[576,576]{1,0:T(8,128)(2,1)}, u32[]{:S(2)}) copy-start(bf16[576,576]{1,0:T(8,128)(2,1)} %param.24) | copy-start | bytes 1990660
  182.4 14.3 %copy-start.9 = (bf16[576,576]{1,0:T(8,128)(2,1)S(1)}, bf16[576,576]{1,0:T(8,128)(2,1)}, u32[]{:S(2)}) copy-start(bf16[576,576]{1,0:T(8,128)(2,1)} %param.23) | copy-start | bytes 1990660
  196.3 2.2 copy-start.5
  198.4 104.7 %all-reduce.7.cloned.1.call-start = ((), (), s32[]{:S(2)}) async-start(), calls=%async_computation.1 | async-start | bytes 491520 | tf_op jit(solution)/shard_map/psum | solution.py:144
  198.5 3.1 copy-start.7
  198.5 3.1 copy-start.4
  232.8 32.6 %copy-start.2 = (bf16[576,576]{1,0:T(8,128)(2,1)S(1)}, bf16[576,576]{1,0:T(8,128)(2,1)}, u32[]{:S(2)}) copy-start(bf16[576,576]{1,0:T(8,128)(2,1)} %param.26) | copy-start | bytes 1990660
  267.4 131.3 %all-reduce.9.cloned.1.call-start = ((), (), s32[]{:S(2)}) async-start(), calls=%async_computation.2 | async-start | bytes 4423680 | tf_op jit(solution)/shard_map/psum | solution.py:155
  319.8 13.7 %copy-start.1 = (bf16[384,4608]{1,0:T(8,128)(2,1)S(1)}, bf16[384,4608]{1,0:T(8,128)(2,1)}, u32[]{:S(2)}) copy-start(bf16[384,4608]{1,0:T(8,128)(2,1)} %select_n.76) | copy-start | bytes 10616836
  343.4 1.7 copy-start.3
  345.1 116.7 %all-reduce.11.cloned.1.call-start = ((), (), s32[]{:S(2)}) async-start(), calls=%async_computation.3 | async-start | bytes 491520 | tf_op jit(solution)/shard_map/psum | solution.py:158
Sparse Core Ops, SparseCore 0:
  198.5 34.2 all-reduce.4
  267.5 35.4 all-reduce.6
  345.2 53.4 all-reduce.8
  426.3 35.3 all-reduce.10

commit v2 on v1

v2 whole, which is shorter than its diff:
```python
import functools
import jax
import jax.numpy as jnp
from jax import lax
from jax.experimental import pallas as pl
from jax.experimental.pallas import tpu as pltpu
from jax.sharding import PartitionSpec as P

EPS = 1e-5
ROPE_BASE = 1.0e6
F32 = jnp.float32
BF16 = jnp.bfloat16
LANES = 128


def dot(a, b):
    return lax.dot_general(a, b, (((1,), (0,)), ((), ())), preferred_element_type=F32)


def dot_nt(a, b):
    return lax.dot_general(a, b, (((1,), (1,)), ((), ())), preferred_element_type=F32)


def gather_kernel(rows, vocab, depth, tok_ref, tok_col, last_ref, emb_ref, x_ref, buf, acc, sem):
    tiles = vocab // LANES

    def copy(i):
        tile = jnp.minimum(tok_ref[i] // LANES, tiles - 1)
        src = emb_ref.at[:, pl.ds(pl.multiple_of(tile * LANES, LANES), LANES)]
        slot = lax.rem(i, depth)
        return pltpu.make_async_copy(src, buf.at[slot], sem.at[slot])

    @pl.loop(0, depth)
    def _(i):
        copy(i).start()

    lane_id = lax.broadcasted_iota(jnp.int32, acc.shape[1:], 1)

    @pl.loop(0, rows)
    def _(i):
        copy(i).wait()
        lane, group = lax.rem(i, LANES), i // LANES
        shift = lax.rem(lane - lax.rem(tok_ref[i], LANES) + LANES, LANES)
        moved = pltpu.roll(buf[lax.rem(i, depth)].astype(acc.dtype), shift, 1)
        acc[group] = jnp.where(lane_id == lane, moved, acc[group])

        @pl.when(i + depth < rows)
        def _():
            copy(i + depth).start()

    groups = pl.cdiv(rows, LANES)
    x_all = jnp.concatenate([acc[g].astype(F32).T for g in range(groups)], axis=0)[:rows]
    x_ref[...] = jnp.where(tok_col[...] >= tiles * LANES, last_ref[...].astype(F32), x_all).astype(BF16)


def gather(emb_table, tokens, acc_dtype=BF16, depth=32):
    vocab, width = emb_table.shape
    rows = tokens.shape[0]
    vmem = pl.BlockSpec(memory_space=pltpu.VMEM)
    tiles = vocab // LANES
    last = lax.slice(emb_table, (vocab - 1, 0), (vocab, width))
    assert vocab - tiles * LANES == 1
    return pl.pallas_call(
        functools.partial(gather_kernel, rows, vocab, depth),
        in_specs=[pl.BlockSpec(memory_space=pltpu.SMEM), vmem, vmem, pl.BlockSpec(memory_space=pl.ANY)],
        out_specs=vmem,
        out_shape=jax.ShapeDtypeStruct((rows, width), BF16),
        scratch_shapes=[pltpu.VMEM((depth, width, LANES), BF16), pltpu.VMEM((pl.cdiv(rows, LANES), width, LANES), acc_dtype), pltpu.SemaphoreType.DMA((depth,))],
        name="gather",
    )(tokens, tokens[:, None], last, emb_table.T)


def attention_kernel(steps, batch, block, heads, head, lens_ref, kvq_ref, cos_ref, sin_ref, swap_ref, k_in, v_in, o_ref, k_out, v_out, q_rows, kt_ref, vt_ref, o_rows):
    cols = heads * head
    slots = k_in.shape[-1]
    rows = steps * batch
    i = pl.program_id(0)
    hpad = 16
    per_group = slots // 4

    @pl.when(i == 0)
    def _():
        cosine, sine = cos_ref[...], sin_ref[...]
        row = lax.broadcasted_iota(jnp.int32, (rows, 4 * batch), 0)
        col = lax.broadcasted_iota(jnp.int32, (rows, 4 * batch), 1)
        perm = jnp.where((row // batch == col % 4) & (row % batch == col // 4), 1.0, 0.0).astype(BF16)
        for part in (2, 0):
            val = kvq_ref[part]
            swapped = dot(val, swap_ref[...])
            rot = (val.astype(F32) * cosine + swapped * sine).astype(BF16).astype(F32)
            if part == 2:
                q_rows[...] = rot.reshape(steps, batch, cols)
            else:
                kt = dot(rot.T.astype(BF16), perm)
        vt = dot(kvq_ref[1].astype(F32).T.astype(BF16), perm)
        for g in range(batch // per_group):
            kt_ref[g] = kt[:, g * slots:(g + 1) * slots].astype(kt_ref.dtype)
            vt_ref[g] = vt[:, g * slots:(g + 1) * slots].astype(vt_ref.dtype)

    head_mask = lax.broadcasted_iota(jnp.int32, (hpad, cols), 1) // head == lax.broadcasted_iota(jnp.int32, (hpad, cols), 0)
    t_of = lax.broadcasted_iota(jnp.int32, (steps * hpad, slots), 0) // hpad
    s_of = lax.broadcasted_iota(jnp.int32, (steps * hpad, slots), 1)
    slot_id = lax.broadcasted_iota(jnp.int32, (cols, slots), 1)

    group = (i * block) // per_group
    news, scores_all = [], []
    for n in range(block):
        b = i * block + n
        first = lens_ref[b]
        shift = lax.rem(first - 4 * lax.rem(b, per_group) + slots, slots)
        fresh = (slot_id >= first) & (slot_id < first + steps)
        k_new = jnp.where(fresh, pltpu.roll(kt_ref[group], shift, 1).astype(BF16), k_in[n].reshape(cols, slots))
        v_new = jnp.where(fresh, pltpu.roll(vt_ref[group], shift, 1).astype(BF16), v_in[n].reshape(cols, slots))
        k_out[n] = k_new.reshape(heads, head, slots)
        v_out[n] = v_new.reshape(heads, head, slots)
        q_blk = jnp.concatenate([jnp.where(head_mask, jnp.broadcast_to(q_rows[t, pl.ds(b, 1), :], (hpad, cols)), 0.0) for t in range(steps)], axis=0).astype(BF16)
        scores = dot(q_blk, k_new) * head ** -0.5
        scores_all.append(jnp.where(s_of <= first + t_of, scores, -1.0e30))
        news.append(v_new)
    scores = jnp.concatenate(scores_all, axis=0)
    peak = jnp.max(scores, axis=-1, keepdims=True)
    weight = jnp.exp(scores - peak)
    total = jnp.sum(weight, axis=-1, keepdims=True)
    weight = weight.astype(BF16)
    span = steps * hpad
    for n in range(block):
        b = i * block + n
        mixed = dot_nt(weight[n * span:(n + 1) * span], news[n]) / total[n * span:(n + 1) * span]
        for t in range(steps):
            o_rows[t, pl.ds(b, 1), :] = jnp.sum(jnp.where(head_mask, mixed[t * hpad:(t + 1) * hpad], 0.0), axis=0, keepdims=True)

    @pl.when(i == pl.num_programs(0) - 1)
    def _():
        o_ref[...] = o_rows[...].reshape(rows, cols).astype(BF16)


def attention(lengths, kvq, cos_t, sin_t, k_cache, v_cache, steps, block=16, roll_dtype=BF16):
    batch, slots, heads, head = k_cache.shape
    cols, rows = heads * head, steps * batch
    k_t, v_t = jnp.transpose(k_cache, (0, 2, 3, 1)), jnp.transpose(v_cache, (0, 2, 3, 1))
    src = jnp.arange(cols)[:, None]
    dst = jnp.arange(cols)[None, :]
    low = dst % head < head // 2
    swap = (jnp.where(low & (src == dst + head // 2), -1.0, 0.0) + jnp.where(~low & (src == dst - head // 2), 1.0, 0.0)).astype(BF16)
    whole = lambda shape: pl.BlockSpec(shape, lambda i: (0,) * len(shape))
    cache_blk = pl.BlockSpec((block, heads, head, slots), lambda i: (i, 0, 0, 0))
    groups = 4 * batch // slots
    o, k_o, v_o = pl.pallas_call(
        functools.partial(attention_kernel, steps, batch, block, heads, head),
        grid=(batch // block,),
        in_specs=[pl.BlockSpec(memory_space=pltpu.SMEM), whole((3, rows, cols)), whole((rows, cols)), whole((rows, cols)), whole((cols, cols)), cache_blk, cache_blk],
        out_specs=[whole((rows, cols)), cache_blk, cache_blk],
        out_shape=[jax.ShapeDtypeStruct((rows, cols), BF16), jax.ShapeDtypeStruct(k_t.shape, BF16), jax.ShapeDtypeStruct(v_t.shape, BF16)],
        scratch_shapes=[pltpu.VMEM((steps, batch, cols), F32), pltpu.VMEM((groups, cols, slots), roll_dtype), pltpu.VMEM((groups, cols, slots), roll_dtype), pltpu.VMEM((steps, batch, cols), F32)],
        compiler_params=pltpu.CompilerParams(dimension_semantics=("arbitrary",)),
        cost_estimate=pl.CostEstimate(flops=4 * 10 ** 9, bytes_accessed=4 * k_t.size * 2, transcendentals=0),
        name="attention",
    )(lengths, kvq, cos_t, sin_t, swap, k_t, v_t)
    back = lambda a: jnp.transpose(a, (0, 3, 1, 2))
    return o, back(k_o), back(v_o)


X, Y = 'x', 'y'
MESH = pl.DeviceIdType.MESH


def positions():
    xi, yi = lax.axis_index(X), lax.axis_index(Y)
    core, chip = lax.rem(xi, 2), xi // 2
    pair = xi + 1 - 2 * core
    cross = lax.rem(xi + 2, 4)
    diag = lax.rem(pair + 2, 4)
    return xi, yi, core, chip, pair, cross, diag


def enter(x_peers, yi, y_count):
    barrier = pltpu.get_barrier_semaphore()
    for peer in x_peers:
        pl.semaphore_signal(barrier, inc=1, device_id={X: peer}, device_id_type=MESH)
    for d in range(1, y_count):
        pl.semaphore_signal(barrier, inc=1, device_id={Y: lax.rem(yi + d, y_count)}, device_id_type=MESH)
    pl.semaphore_wait(barrier, len(x_peers) + y_count - 1)


def remote(src, dst, send, recv, **where):
    return pltpu.make_async_remote_copy(src_ref=src, dst_ref=dst, send_sem=send, recv_sem=recv, device_id=where, device_id_type=MESH)


def start_all(copies):
    for c in copies:
        c.start()
    return copies


def scatter_y(src, dst, sems, yi, y_count, span):
    out = []
    for d in range(1, y_count):
        peer = lax.rem(yi + d, y_count)
        rows = pl.ds(pl.multiple_of(peer * span, span), span)
        out.append(remote(src.at[rows], dst.at[d - 1], sems.at[0, d - 1], sems.at[1, d - 1], y=peer))
    return start_all(out)


def gather_y(src, dst, sems, yi, y_count, span):
    rows = pl.ds(pl.multiple_of(yi * span, span), span)
    return start_all([remote(src, dst.at[rows], sems.at[0, d - 1], sems.at[1, d - 1], y=lax.rem(yi + d, y_count)) for d in range(1, y_count)])


def normalise(x_f32, gain, stat, stat_in, sems, peers, width_full):
    rows = x_f32.shape[0]
    part = jnp.sum(x_f32 * x_f32, axis=-1, keepdims=True)
    stat[:, :rows] = jnp.broadcast_to(part, (rows, LANES)).T[:8]
    copies = start_all([remote(stat, stat_in.at[i], sems.at[0, i], sems.at[1, i], x=peer) for i, peer in enumerate(peers)])
    for c in copies:
        c.wait()
    total = ((stat[...] + stat_in[0]) + (stat_in[1] + stat_in[2])).T[:rows, :1]
    return (x_f32 * lax.rsqrt(total / width_full + EPS) * gain).astype(BF16)


def qkv_kernel(y_count, width_full, x_ref, g_ref, wk_ref, wv_ref, wq_ref, out_ref, stat, stat_in, h_own, h_all, keep, snd1, rcv1, snd2, rcv2, done, rcv3, stat_sem, y_sem, s1, s2, s3):
    xi, yi, core, chip, pair, cross, diag = positions()
    span, rows = x_ref.shape[0], h_all.shape[0]
    half = rows // 2
    stat[...] = jnp.zeros_like(stat)
    enter((pair, cross, diag), yi, y_count)
    h = normalise(x_ref[...].astype(F32), g_ref[...].astype(F32), stat, stat_in, stat_sem, (pair, cross, diag), width_full)
    h_own[...] = h
    sent = gather_y(h_own, h_all, y_sem, yi, y_count, span)
    h_all[pl.ds(pl.multiple_of(yi * span, span), span)] = h
    for c in sent:
        c.wait()
    mine = pl.ds(pl.multiple_of(core * half, half), half)
    theirs = pl.ds(pl.multiple_of((1 - core) * half, half), half)
    first, second, third = [], [], []
    weights = (wk_ref, wv_ref, wq_ref)
    for m in range(3):
        snd1[m] = dot(h_all[theirs], weights[m][...]).astype(BF16)
        first += start_all([remote(snd1.at[m], rcv1.at[m], s1.at[0, m], s1.at[1, m], x=pair)])
        keep[m] = dot(h_all[mine], weights[m][...])
        first[m].wait_recv()
        snd2[m] = (keep[m] + rcv1[m].astype(F32)).astype(BF16)
        second += start_all([remote(snd2.at[m], rcv2.at[m], s2.at[0, m], s2.at[1, m], x=cross)])
    for m in range(3):
        second[m].wait_recv()
        done[m] = (snd2[m].astype(F32) + rcv2[m].astype(F32)).astype(BF16)
        third += start_all([remote(done.at[m], rcv3.at[m], s3.at[0, m], s3.at[1, m], x=pair)])
        out_ref[m, mine] = done[m]
    for m in range(3):
        third[m].wait_recv()
        out_ref[m, theirs] = rcv3[m]
    for c in first + second + third:
        c.wait_send()


def qkv_sums(x_own, gain, w_q, w_k, w_v, rows, y_count, width_full):
    span, width = x_own.shape
    cols, half = w_q.shape[1], rows // 2
    vmem = pl.BlockSpec(memory_space=pltpu.VMEM)
    part = pltpu.VMEM((3, half, cols), BF16)
    pairs = pltpu.SemaphoreType.DMA((2, 3))
    return pl.pallas_call(
        functools.partial(qkv_kernel, y_count, width_full),
        in_specs=[vmem] * 5,
        out_specs=vmem,
        out_shape=jax.ShapeDtypeStruct((3, rows, cols), BF16),
        scratch_shapes=[pltpu.VMEM((8, LANES), F32), pltpu.VMEM((3, 8, LANES), F32), pltpu.VMEM((span, width), BF16), pltpu.VMEM((rows, width), BF16), pltpu.VMEM((3, half, cols), F32), part, part, part, part, part, part, pairs, pltpu.SemaphoreType.DMA((2, y_count - 1)), pairs, pairs, pairs],
        compiler_params=pltpu.CompilerParams(collective_id=0, has_side_effects=True),
        cost_estimate=pl.CostEstimate(flops=6 * rows * width * cols, bytes_accessed=8 * width * cols, transcendentals=0),
        name="qkv_sums",
    )(x_own, gain[None, :], w_k, w_v, w_q)


def chunks_of(ff, wide):
    return tuple((lo, min(wide, ff - lo)) for lo in range(0, ff, wide))


def moe_kernel(y_count, width_full, chunks, experts, o_ref, wo_ref, x_ref, g_ref, wr_ref, ch_ref, act_hbm, lin_hbm, down_hbm, out_ref, act, lin, down, stat, stat_in, part, rs_in, h_own, h_all, logit, logit_in, gate, mask, sparse, acc_down, x_mid, *rest):
    n_chunk = len(chunks)
    keep, snd1, rcv1, snd2, rcv2, u_mine, u_pair = [rest[i * n_chunk:(i + 1) * n_chunk] for i in range(7)]
    w_sem, stat_sem, rs_sem, ag_sem, lg_sem, s1, s2, s3, s4, s5, rs2_sem, ag2_sem = rest[7 * n_chunk:]
    xi, yi, core, chip, pair, cross, diag = positions()
    peers = (pair, cross, diag)
    span, rows = x_ref.shape[0], h_all.shape[0]
    half, width = rows // 2, x_ref.shape[1]
    loads = []
    for i, (src, dst) in enumerate(((act_hbm, act), (lin_hbm, lin), (down_hbm, down))):
        for e in range(experts):
            loads.append(pltpu.make_async_copy(src.at[e], dst.at[e], w_sem.at[i, e]))
    start_all(loads)
    stat[...] = jnp.zeros_like(stat)
    logit[...] = jnp.zeros_like(logit)
    enter(peers, yi, y_count)

    own = pl.ds(pl.multiple_of(yi * span, span), span)
    part[...] = dot(o_ref[...], wo_ref[...]).astype(BF16)
    sent = scatter_y(part, rs_in, rs_sem, yi, y_count, span)
    ch = ch_ref[...]
    ch_keep = jnp.where(core == 0, ch[:, :1], ch[:, 1:])
    ch_send = jnp.where(core == 0, ch[:, 1:], ch[:, :1])
    for e in range(experts):
        mask[0, e] = jnp.broadcast_to(jnp.where(ch_keep == e, 1.0, 0.0), (rows, LANES)).astype(BF16)
        mask[1, e] = jnp.broadcast_to(jnp.where(ch_send == e, 1.0, 0.0), (rows, LANES)).astype(BF16)

    def wide_mask(s, e, n):
        return jnp.concatenate([mask[s, e]] * (n // LANES) + ([mask[s, e][:, :n % LANES]] if n % LANES else []), axis=1)

    for c in sent:
        c.wait()
    total = part[own].astype(F32) + rs_in[0].astype(F32) + rs_in[1].astype(F32) + rs_in[2].astype(F32)
    x_new = (x_ref[...].astype(F32) + total).astype(BF16)
    x_mid[...] = x_new
    h = normalise(x_new.astype(F32), g_ref[...].astype(F32), stat, stat_in, stat_sem, peers, width_full)
    h_own[...] = h
    sent = gather_y(h_own, h_all, ag_sem, yi, y_count, span)
    h_all[own] = h
    for c in sent:
        c.wait()
    logit[:, :rows] = dot_nt(wr_ref[...], h_all[...])
    lg = start_all([remote(logit, logit_in.at[i], lg_sem.at[0, i], lg_sem.at[1, i], x=peer) for i, peer in enumerate(peers)])
    h2 = h_all[...]
    for e in range(experts):
        for s in range(2):
            sparse[s, e] = h2 * wide_mask(s, e, width)

    for copy in loads[:2 * experts]:
        copy.wait()

    mine = pl.ds(pl.multiple_of(chip * half, half), half)
    other = pl.ds(pl.multiple_of((1 - chip) * half, half), half)
    first, second, to_cross, to_pair, forward = [], [], [], [], []

    def product(s, w, lo, n):
        def body(e, acc):
            return acc + dot(sparse[s, e], w[e, :, lo:lo + n])
        return lax.fori_loop(0, experts, body, jnp.zeros((rows, n), F32))

    def sums(k):
        lo, n = chunks[k]
        snd1[k][0] = product(1, act, lo, n).astype(BF16)
        snd1[k][1] = product(1, lin, lo, n).astype(BF16)
        first.extend(start_all([remote(snd1[k], rcv1[k], s1.at[0, k], s1.at[1, k], x=pair)]))
        keep[k][0] = product(0, act, lo, n)
        keep[k][1] = product(0, lin, lo, n)
        first[k].wait_recv()
        for i in range(2):
            snd2[k][i] = (keep[k][i, other] + rcv1[k][i, other].astype(F32)).astype(BF16)
        second.extend(start_all([remote(snd2[k], rcv2[k], s2.at[0, k], s2.at[1, k], x=cross)]))
        for i in range(2):
            keep[k][i, mine] = keep[k][i, mine] + rcv1[k][i, mine].astype(F32)

    def gates():
        for c in lg:
            c.wait()
        logits = ((logit[...] + logit_in[0]) + (logit_in[1] + logit_in[2])).T[:rows]
        col = lax.broadcasted_iota(jnp.int32, logits.shape, 1)
        l_keep = jnp.sum(jnp.where(col == ch_keep, logits, 0.0), axis=1, keepdims=True)
        l_send = jnp.sum(jnp.where(col == ch_send, logits, 0.0), axis=1, keepdims=True)
        top = jnp.maximum(l_keep, l_send)
        e_keep, e_send = jnp.exp(l_keep - top), jnp.exp(l_send - top)
        gate[...] = jnp.broadcast_to(e_keep / (e_keep + e_send), gate.shape)

    def unit(k):
        second[k].wait_recv()
        a = keep[k][0, mine] + rcv2[k][0].astype(F32)
        b = keep[k][1, mine] + rcv2[k][1].astype(F32)
        u_mine[k][mine] = (gate[mine][:, :1] * (a * jax.nn.sigmoid(a)) * b).astype(BF16)
        to_cross.extend(start_all([remote(u_mine[k].at[mine], u_mine[k].at[mine], s3.at[0, k], s3.at[1, k], x=cross)]))
        to_pair.extend(start_all([remote(u_mine[k].at[mine], u_pair[k].at[mine], s4.at[0, k], s4.at[1, k], x=pair)]))

    def pass_on(k):
        to_cross[k].wait_recv()
        forward.extend(start_all([remote(u_mine[k].at[other], u_pair[k].at[other], s5.at[0, k], s5.at[1, k], x=pair)]))

    def downward(k):
        lo, n = chunks[k]
        to_pair[k].wait_recv()
        forward[k].wait_recv()
        u0, u1 = u_mine[k][...], u_pair[k][...]
        total = jnp.zeros((rows, width), F32) if k == 0 else acc_down[...]
        for e in range(experts):
            total = total + dot_nt(u0 * wide_mask(0, e, n) + u1 * wide_mask(1, e, n), down[e, :, lo:lo + n])
        acc_down[...] = total

    sums(0)
    sums(1)
    gates()
    sums(2)
    unit(0)
    for k in range(3, n_chunk):
        sums(k)
    unit(1)
    pass_on(0)
    for copy in loads[2 * experts:]:
        copy.wait()
    for k in range(2, n_chunk):
        unit(k)
        pass_on(k - 1)
        downward(k - 2)
    pass_on(n_chunk - 1)
    downward(n_chunk - 2)
    downward(n_chunk - 1)

    part[...] = acc_down[...].astype(BF16)
    sent = scatter_y(part, rs_in, rs2_sem, yi, y_count, span)
    for c in sent:
        c.wait()
    total = part[own].astype(F32) + rs_in[0].astype(F32) + rs_in[1].astype(F32) + rs_in[2].astype(F32)
    h_new = (x_mid[...].astype(F32) + total).astype(BF16)
    h_own[...] = h_new
    sent = gather_y(h_own, h_all, ag2_sem, yi, y_count, span)
    h_all[own] = h_new
    for c in sent:
        c.wait()
    out_ref[...] = h_all[...]
    for c in first + second + to_cross + to_pair + forward:
        c.wait_send()


def moe(mixed, w_o, x_own, gain, w_router, choice, w_act, w_lin, w_down, y_count, width_full):
    rows, heads = mixed.shape
    span, width = x_own.shape
    experts, _, ff = w_act.shape
    half, chunks = rows // 2, chunks_of(ff, 384)
    vmem, hbm = pl.BlockSpec(memory_space=pltpu.VMEM), pl.BlockSpec(memory_space=pl.ANY)
    down_t = jnp.transpose(w_down, (0, 2, 1))
    three = pltpu.SemaphoreType.DMA((2, 3))
    ring = pltpu.SemaphoreType.DMA((2, y_count - 1))
    per_chunk = pltpu.SemaphoreType.DMA((2, len(chunks)))
    buf = lambda lead, r, dt: [pltpu.VMEM(lead + (r, n), dt) for _, n in chunks]
    scratch = [pltpu.VMEM(w_act.shape, BF16), pltpu.VMEM(w_act.shape, BF16), pltpu.VMEM(down_t.shape, BF16), pltpu.VMEM((8, LANES), F32), pltpu.VMEM((3, 8, LANES), F32), pltpu.VMEM((rows, width), BF16), pltpu.VMEM((y_count - 1, span, width), BF16), pltpu.VMEM((span, width), BF16), pltpu.VMEM((rows, width), BF16), pltpu.VMEM((experts, 2 * LANES), F32), pltpu.VMEM((3, experts, 2 * LANES), F32), pltpu.VMEM((rows, LANES), F32), pltpu.VMEM((2, experts, rows, LANES), BF16), pltpu.VMEM((2, experts, rows, width), BF16), pltpu.VMEM((rows, width), F32), pltpu.VMEM((span, width), BF16)]
    scratch += buf((2,), rows, F32) + buf((2,), rows, BF16) + buf((2,), rows, BF16) + buf((2,), half, BF16) + buf((2,), half, BF16) + buf((), rows, BF16) + buf((), rows, BF16)
    scratch += [pltpu.SemaphoreType.DMA((3, experts)), three, ring, ring, three] + [per_chunk] * 5 + [ring, ring]
    return pl.pallas_call(
        functools.partial(moe_kernel, y_count, width_full, chunks, experts),
        in_specs=[vmem] * 6 + [hbm] * 3,
        out_specs=vmem,
        out_shape=jax.ShapeDtypeStruct((rows, width), BF16),
        scratch_shapes=scratch,
        compiler_params=pltpu.CompilerParams(collective_id=1, has_side_effects=True, vmem_limit_bytes=67043328),
        cost_estimate=pl.CostEstimate(flops=2 * 10 ** 10, bytes_accessed=6 * w_act.size, transcendentals=0),
        name="moe",
    )(mixed, w_o, x_own, gain[None, :], w_router.T, choice, w_act, w_lin, down_t)


def rope_tables(lengths, steps, heads, head):
    half = head // 2
    inv_freq = ROPE_BASE ** (-(jnp.arange(half, dtype=F32) * 2.0 / head))
    spots = (lengths[None, :] + jnp.arange(steps)[:, None]).reshape(-1).astype(F32)
    angles = spots[:, None] * inv_freq[None, :]
    tile = lambda a: jnp.concatenate([a] * (2 * heads), axis=1)
    return tile(jnp.cos(angles)), tile(jnp.sin(angles))


def solution(mesh):
    x_count, y_count = mesh.shape['x'], mesh.shape['y']
    assert x_count == 4 and y_count == 4
    cache_spec = P('dp', None, 'y', None)
    in_specs = (P(None, 'dp'), P('dp'), P(None, 'dp', None), P(None, 'x'), cache_spec, cache_spec, P('x'), P('x', 'y'), P('x', 'y'), P('x', 'y'), P('y', 'x'), P('x'), P('x', None), P(None, 'x', 'y'), P(None, 'x', 'y'), P(None, 'y', 'x'))
    out_specs = (P(None, 'dp', 'x'), cache_spec, cache_spec)

    def per_device(tokens, lengths, choices, emb_table, k_cache, v_cache, g_attn, w_q, w_k, w_v, w_o, g_ffn, w_router, w_act, w_lin, w_down):
        steps, n_batch = tokens.shape
        heads, head = k_cache.shape[2], k_cache.shape[3]
        rows = steps * n_batch
        width_full = emb_table.shape[1] * x_count
        span = rows // y_count
        cos_t, sin_t = rope_tables(lengths, steps, heads, head)
        own_tokens = lax.dynamic_slice(tokens.reshape(rows), (lax.axis_index('y') * span,), (span,))
        x_own = gather(emb_table, own_tokens)
        kvq = qkv_sums(x_own, g_attn, w_q, w_k, w_v, rows, y_count, width_full)
        mixed, k_out, v_out = attention(lengths, kvq, cos_t, sin_t, k_cache, v_cache, steps)
        out = moe(mixed, w_o, x_own, g_ffn, w_router, choices.reshape(rows, 2), w_act, w_lin, w_down, y_count, width_full)
        return out.reshape(steps, n_batch, emb_table.shape[1]), k_out, v_out

    return jax.shard_map(per_device, mesh=mesh, in_specs=in_specs, out_specs=out_specs, check_vma=False)
```

time: 475 us -> 161 us (0.34)
  local copies, waits for them, and re-layouts: 200 us -> 10.1 us
  waiting for transfers between devices: 147 us -> 0 us
  Pallas kernels: 32.6 us -> 148 us
  matrix products: 39.4 us -> 0 us
  blocking collectives: 21.3 us -> 0 us
  other arithmetic: 15.5 us -> 2 us
  between operations: 14 us -> 0.7 us
    unnamed x22 -> x11, local copies, waits for them, and re-layouts: 174 us -> 3.14 us
    psum x4 -> x0, waiting for transfers between devices: 147 us -> none  [the longest x1 46.3 us: per_device(): hid = lax.psum(hid_part, 'x').astype(F32)]
    pallas_call x0 -> x3, Pallas kernels: none -> 128 us  [the longest x1 91.4 us: moe(): pl.pallas_call(functools.partial(moe_kernel, y_count, width_full, chunks,...]
    dot_general x8 -> x0, matrix products: 39.4 us -> none  [the longest x7 27.1 us: dot(): lax.dot_general(a, b, (((1,), (0,)), ((), ())), preferred_element_type=F32)]
    psum x3 -> x0, blocking collectives: 21.3 us -> none  [the longest x2 14.3 us: shard_norm(): sq_total = lax.psum(jnp.sum(x_f32 * x_f32, axis=-1, keepdims=True), 'x')]
    pallas_call x1, Pallas kernels: 32.6 us -> 19.5 us  [attention(): pl.pallas_call(functools.partial(attention_kernel, steps, batch, block, h...]
    slice x3 -> x1, local copies, waits for them, and re-layouts: 9.09 us -> 0.92 us  [gather(): last = lax.slice(emb_table, (vocab - 1, 0), (vocab, width))]
    select_n x1 -> x0, local copies, waits for them, and re-layouts: 7.19 us -> none  [per_device(): jnp.where(hot_t[..., None], normed2[None, :, None, :], 0)]
  transfers between devices with their start and end apart: 4 -> 0, of which waited for: 4 -> 0; matrix products, arithmetic and copies ran while one was open for 1% -> 0% of each run, Pallas kernels for 0% -> 0%
where the time goes in v2:
time: 161 us
  Pallas kernels  148 us (92%)
  local copies, waits for them, and re-layouts  10.1 us (6%)
  other arithmetic  2 us (1%)
    pallas_call x1, Pallas kernels, moe(): pl.pallas_call(functools.partial(moe_kernel, y_count, width_full, chunks,...  91.4 us
    pallas_call x1, Pallas kernels, qkv_sums(): pl.pallas_call(functools.partial(qkv_kernel, y_count, width_full), in_spe...  28.5 us
    pallas_call x1, Pallas kernels, attention(): pl.pallas_call(functools.partial(attention_kernel, steps, batch, block, h...  19.5 us
    pallas_call x1, Pallas kernels, gather(): pl.pallas_call(functools.partial(gather_kernel, rows, vocab, depth), in_s...  8.33 us

profile of v2, /device:TPU:0, one launch (start us, length us, event | category | flops | bytes accessed | tf_op | source)
XLA Modules:
  0.0 160.6 jit_solution(16424354272091946558)
XLA Ops:
  0.6 0.8 reshape.67
  1.4 0.1 dynamic-slice_bitcast_fusion
  1.5 0.7 copy.20.tok_col
  2.2 0.6 dynamic_slice.3.tok_ref
  2.8 0.9 slice.3
  3.7 0.7 copy.22.last_ref
  4.4 0.0 copy-start.2
  4.4 8.3 %gather.1.x_ref = bf16[48,576]{1,0:T(8,128)(2,1)} custom-call(s32[48]{0:T(128)} %dynamic_slice.3.tok_ref, s32[48,1]{1,0:T(8,128)} %copy.20.tok_col, bf16[1,576]{1,0:T(2,128)(2,1)} %copy.22.last_ref, bf16[576,122753]{1,0:T(8,128)(2,1)} %bitcast.1.emb_ref), custom_call_target="tpu_custom_call" | custom-call | tf_op jit(solution)/shard_map/gather/pallas_call | solution.py:63
  12.7 0.0 copy-done.2
  12.7 0.6 broadcast_in_dim.28.g_ref
  13.3 28.5 %qkv_sums.1.kvq_ref = bf16[3,192,576]{2,1,0:T(8,128)(2,1)} custom-call(bf16[48,576]{1,0:T(8,128)(2,1)} %gather.1.x_ref, bf16[1,576]{1,0:T(2,128)(2,1)} %broadcast_in_dim.28.g_ref, bf16[576,576]{1,0:T(8,128)(2,1)} %wk_ref.1, bf16[576,576]{1,0:T(8,128)(2,1)} %wv_ref.1, bf16[576,576]{1,0:T(8,128)(2,1)} %wq_ref.1), custom_call_target="tpu_custom_call" | custom-call | flops 382205952 | bytes 2654208 | tf_op jit(solution)/shard_map/qkv_sums/pallas_call | solution.py:261
  41.9 1.6 add_convert_fusion.swap_ref
  43.5 0.0 copy-done.1
  43.5 0.1 convert_element_type.14
  43.6 0.4 multiply_sine_fusion
  44.0 1.3 concatenate.6.cos_ref
  45.3 1.3 concatenate.7.sin_ref
  46.6 19.5 %attention.1 = (bf16[192,576]{1,0:T(8,128)(2,1)}, bf16[64,9,64,128]{3,2,1,0:T(8,128)(2,1)}, bf16[64,9,64,128]{3,2,1,0:T(8,128)(2,1)}) custom-call(s32[64]{0:T(128)} %lens_ref.1, bf16[3,192,576]{2,1,0:T(8,128)(2,1)} %qkv_sums.1.kvq_ref, f32[192,576]{1,0:T(8,128)} %concatenate.6.cos_ref, f32[192,576]{1,0:T(8,128)} %concatenate.7.sin_ref, ...), custom_call_target="tpu_custom_call" | custom-call | flops 4000000000 | bytes 37748736 | tf_op jit(solution)/shard_map/attention/pallas_call | solution.py:148
  66.2 0.0 copy-done
  66.2 0.8 copy.21
  66.9 0.0 copy-done.3
  66.9 0.6 broadcast_in_dim.32.g_ref
  67.5 91.4 %moe.1 = bf16[192,576]{1,0:T(8,128)(2,1)} custom-call(bf16[192,576]{1,0:T(8,128)(2,1)} %get-tuple-element.6.o_ref, bf16[576,576]{1,0:T(8,128)(2,1)} %wo_ref.1, bf16[48,576]{1,0:T(8,128)(2,1)} %gather.1.x_ref, bf16[1,576]{1,0:T(2,128)(2,1)} %broadcast_in_dim.32.g_ref, bf16[8,576]{1,0:T(8,128)(2,1)} %bitcast.18, s32[192,2]{1,0:T(8,128)} %bitcast.14, ...), custom_call_target="tpu_custom_call" | custom-call | flops 20000000000 | bytes 39813120 | tf_op jit(solution)/shard_map/moe/pallas_call | solution.py:433
  158.9 1.7 %copy.24 = bf16[3,64,576]{2,1,0:T(8,128)(2,1)} copy(bf16[3,64,576]{2,1,0:T(8,128)(2,1)} %bitcast.13) | data formatting | bytes 442368
  (7 shorter events, 0.0 us)
Async XLA Ops:
  4.4 8.3 %copy-start.2 = (bf16[576]{0:T(1024)(128)(2,1)S(1)}, bf16[576]{0:T(1024)(128)(2,1)}, u32[]{:S(2)}) copy-start(bf16[576]{0:T(1024)(128)(2,1)} %param.22) | copy-start | bytes 3460
  13.3 30.1 %copy-start.1 = (s32[64]{0:T(128)S(1)}, s32[64]{0:T(128)}, u32[]{:S(2)}) copy-start(s32[64]{0:T(128)} %lens_ref.1) | copy-start | bytes 772
  46.6 19.5 %copy-start = (s32[3,64,2]{1,2,0:T(2,128)S(1)}, s32[3,64,2]{1,2,0:T(2,128)}, u32[]{:S(2)}) copy-start(s32[3,64,2]{1,2,0:T(2,128)} %param.18) | copy-start | bytes 4612
  46.6 20.3 %copy-start.3 = (bf16[576]{0:T(1024)(128)(2,1)S(1)}, bf16[576]{0:T(1024)(128)(2,1)}, u32[]{:S(2)}) copy-start(bf16[576]{0:T(1024)(128)(2,1)} %param.27) | copy-start | bytes 3460

commit v3 on v2

--- a/solution.py
+++ b/solution.py
@@ -21,56 +21,58 @@
     return lax.dot_general(a, b, (((1,), (1,)), ((), ())), preferred_element_type=F32)
 
 
-def gather_kernel(rows, vocab, depth, tok_ref, tok_col, last_ref, emb_ref, x_ref, buf, acc, sem):
+def gather_kernel(span, vocab, depth, tok_ref, edge_ref, emb_ref, x_ref, buf, acc, sem):
     tiles = vocab // LANES
+    batch = tok_ref.shape[1]
+    start = lax.axis_index('y') * span
+
+    def token(i):
+        r = start + i
+        return tok_ref[r // batch, lax.rem(r, batch)]
 
     def copy(i):
-        tile = jnp.minimum(tok_ref[i] // LANES, tiles - 1)
+        tile = jnp.minimum(token(i) // LANES, tiles - 1)
         src = emb_ref.at[:, pl.ds(pl.multiple_of(tile * LANES, LANES), LANES)]
         slot = lax.rem(i, depth)
         return pltpu.make_async_copy(src, buf.at[slot], sem.at[slot])
 
-    @pl.loop(0, depth)
+    @pl.loop(0, min(depth, span))
     def _(i):
         copy(i).start()
 
-    lane_id = lax.broadcasted_iota(jnp.int32, acc.shape[1:], 1)
-
-    @pl.loop(0, rows)
+    lane_id = lax.broadcasted_iota(jnp.int32, acc.shape, 1)
+
+    @pl.loop(0, span)
     def _(i):
         copy(i).wait()
-        lane, group = lax.rem(i, LANES), i // LANES
-        shift = lax.rem(lane - lax.rem(tok_ref[i], LANES) + LANES, LANES)
-        moved = pltpu.roll(buf[lax.rem(i, depth)].astype(acc.dtype), shift, 1)
-        acc[group] = jnp.where(lane_id == lane, moved, acc[group])
-
-        @pl.when(i + depth < rows)
+        tok = token(i)
+        shift = lax.rem(i - lax.rem(tok, LANES) + LANES, LANES)
+        edge = jnp.full(acc.shape, tok, jnp.int32) >= tiles * LANES
+        moved = pltpu.roll(jnp.where(edge, edge_ref[...], buf[lax.rem(i, depth)]), shift, 1)
+        acc[...] = jnp.where(lane_id == i, moved, acc[...])
+
+        @pl.when(i + depth < span)
         def _():
             copy(i + depth).start()
 
-    groups = pl.cdiv(rows, LANES)
-    x_all = jnp.concatenate([acc[g].astype(F32).T for g in range(groups)], axis=0)[:rows]
-    x_ref[...] = jnp.where(tok_col[...] >= tiles * LANES, last_ref[...].astype(F32), x_all).astype(BF16)
-
-
-def gather(emb_table, tokens, acc_dtype=BF16, depth=32):
+    x_ref[...] = acc[...].astype(F32).T[:span].astype(BF16)
+
+
+def gather(emb_table, tokens, span, depth=48):
     vocab, width = emb_table.shape
-    rows = tokens.shape[0]
-    vmem = pl.BlockSpec(memory_space=pltpu.VMEM)
-    tiles = vocab // LANES
-    last = lax.slice(emb_table, (vocab - 1, 0), (vocab, width))
-    assert vocab - tiles * LANES == 1
+    table = emb_table.T
     return pl.pallas_call(
-        functools.partial(gather_kernel, rows, vocab, depth),
-        in_specs=[pl.BlockSpec(memory_space=pltpu.SMEM), vmem, vmem, pl.BlockSpec(memory_space=pl.ANY)],
-        out_specs=vmem,
-        out_shape=jax.ShapeDtypeStruct((rows, width), BF16),
-        scratch_shapes=[pltpu.VMEM((depth, width, LANES), BF16), pltpu.VMEM((pl.cdiv(rows, LANES), width, LANES), acc_dtype), pltpu.SemaphoreType.DMA((depth,))],
+        functools.partial(gather_kernel, span, vocab, depth),
+        grid=(1,),
+        in_specs=[pl.BlockSpec(memory_space=pltpu.SMEM), pl.BlockSpec((width, LANES), lambda i: (0, vocab // LANES)), pl.BlockSpec(memory_space=pl.ANY)],
+        out_specs=pl.BlockSpec((span, width), lambda i: (0, 0)),
+        out_shape=jax.ShapeDtypeStruct((span, width), BF16),
+        scratch_shapes=[pltpu.VMEM((depth, width, LANES), BF16), pltpu.VMEM((width, LANES), BF16), pltpu.SemaphoreType.DMA((depth,))],
         name="gather",
-    )(tokens, tokens[:, None], last, emb_table.T)
-
-
-def attention_kernel(steps, batch, block, heads, head, lens_ref, kvq_ref, cos_ref, sin_ref, swap_ref, k_in, v_in, o_ref, k_out, v_out, q_rows, kt_ref, vt_ref, o_rows):
+    )(tokens, table, table)
+
+
+def attention_kernel(steps, batch, block, heads, head, lens_ref, kvq_ref, cos_ref, sin_ref, k_in, v_in, o_ref, k_out, v_out, q_rows, kt_ref, vt_ref, o_rows):
     cols = heads * head
     slots = k_in.shape[-1]
     rows = steps * batch
@@ -80,13 +82,21 @@
 
     @pl.when(i == 0)
     def _():
-        cosine, sine = cos_ref[...], sin_ref[...]
+        def spread(table):
+            four = jnp.concatenate([table] * (LANES // table.shape[1]), axis=1)
+            return jnp.concatenate([four] * (cols // LANES) + [four[:, :cols % LANES]], axis=1)
+
+        cosine, sine = spread(cos_ref[...]), spread(sin_ref[...])
+        src = lax.broadcasted_iota(jnp.int32, (cols, cols), 0)
+        dst = lax.broadcasted_iota(jnp.int32, (cols, cols), 1)
+        low = dst % head < head // 2
+        swap = jnp.where(low & (src == dst + head // 2), -1.0, jnp.where(~low & (src == dst - head // 2), 1.0, 0.0)).astype(BF16)
         row = lax.broadcasted_iota(jnp.int32, (rows, 4 * batch), 0)
         col = lax.broadcasted_iota(jnp.int32, (rows, 4 * batch), 1)
         perm = jnp.where((row // batch == col % 4) & (row % batch == col // 4), 1.0, 0.0).astype(BF16)
         for part in (2, 0):
             val = kvq_ref[part]
-            swapped = dot(val, swap_ref[...])
+            swapped = dot(val, swap)
             rot = (val.astype(F32) * cosine + swapped * sine).astype(BF16).astype(F32)
             if part == 2:
                 q_rows[...] = rot.reshape(steps, batch, cols)
@@ -138,24 +148,20 @@
     batch, slots, heads, head = k_cache.shape
     cols, rows = heads * head, steps * batch
     k_t, v_t = jnp.transpose(k_cache, (0, 2, 3, 1)), jnp.transpose(v_cache, (0, 2, 3, 1))
-    src = jnp.arange(cols)[:, None]
-    dst = jnp.arange(cols)[None, :]
-    low = dst % head < head // 2
-    swap = (jnp.where(low & (src == dst + head // 2), -1.0, 0.0) + jnp.where(~low & (src == dst - head // 2), 1.0, 0.0)).astype(BF16)
     whole = lambda shape: pl.BlockSpec(shape, lambda i: (0,) * len(shape))
     cache_blk = pl.BlockSpec((block, heads, head, slots), lambda i: (i, 0, 0, 0))
     groups = 4 * batch // slots
     o, k_o, v_o = pl.pallas_call(
         functools.partial(attention_kernel, steps, batch, block, heads, head),
         grid=(batch // block,),
-        in_specs=[pl.BlockSpec(memory_space=pltpu.SMEM), whole((3, rows, cols)), whole((rows, cols)), whole((rows, cols)), whole((cols, cols)), cache_blk, cache_blk],
+        in_specs=[pl.BlockSpec(memory_space=pltpu.SMEM), whole((3, rows, cols)), whole((rows, head // 2)), whole((rows, head // 2)), cache_blk, cache_blk],
         out_specs=[whole((rows, cols)), cache_blk, cache_blk],
         out_shape=[jax.ShapeDtypeStruct((rows, cols), BF16), jax.ShapeDtypeStruct(k_t.shape, BF16), jax.ShapeDtypeStruct(v_t.shape, BF16)],
         scratch_shapes=[pltpu.VMEM((steps, batch, cols), F32), pltpu.VMEM((groups, cols, slots), roll_dtype), pltpu.VMEM((groups, cols, slots), roll_dtype), pltpu.VMEM((steps, batch, cols), F32)],
         compiler_params=pltpu.CompilerParams(dimension_semantics=("arbitrary",)),
         cost_estimate=pl.CostEstimate(flops=4 * 10 ** 9, bytes_accessed=4 * k_t.size * 2, transcendentals=0),
         name="attention",
-    )(lengths, kvq, cos_t, sin_t, swap, k_t, v_t)
+    )(lengths, kvq, cos_t, sin_t, k_t, v_t)
     back = lambda a: jnp.transpose(a, (0, 3, 1, 2))
     return o, back(k_o), back(v_o)
 
@@ -223,7 +229,7 @@
     half = rows // 2
     stat[...] = jnp.zeros_like(stat)
     enter((pair, cross, diag), yi, y_count)
-    h = normalise(x_ref[...].astype(F32), g_ref[...].astype(F32), stat, stat_in, stat_sem, (pair, cross, diag), width_full)
+    h = normalise(x_ref[...].astype(F32), g_ref[...].astype(F32)[None, :], stat, stat_in, stat_sem, (pair, cross, diag), width_full)
     h_own[...] = h
     sent = gather_y(h_own, h_all, y_sem, yi, y_count, span)
     h_all[pl.ds(pl.multiple_of(yi * span, span), span)] = h
@@ -267,7 +273,7 @@
         compiler_params=pltpu.CompilerParams(collective_id=0, has_side_effects=True),
         cost_estimate=pl.CostEstimate(flops=6 * rows * width * cols, bytes_accessed=8 * width * cols, transcendentals=0),
         name="qkv_sums",
-    )(x_own, gain[None, :], w_k, w_v, w_q)
+    )(x_own, gain, w_k, w_v, w_q)
 
 
 def chunks_of(ff, wide):
@@ -285,7 +291,8 @@
     loads = []
     for i, (src, dst) in enumerate(((act_hbm, act), (lin_hbm, lin), (down_hbm, down))):
         for e in range(experts):
-            loads.append(pltpu.make_async_copy(src.at[e], dst.at[e], w_sem.at[i, e]))
+            place = dst.at[e] if i == 2 else dst.at[pl.ds(e * width, width)]
+            loads.append(pltpu.make_async_copy(src.at[e], place, w_sem.at[i, e]))
     start_all(loads)
     stat[...] = jnp.zeros_like(stat)
     logit[...] = jnp.zeros_like(logit)
@@ -294,9 +301,10 @@
     own = pl.ds(pl.multiple_of(yi * span, span), span)
     part[...] = dot(o_ref[...], wo_ref[...]).astype(BF16)
     sent = scatter_y(part, rs_in, rs_sem, yi, y_count, span)
-    ch = ch_ref[...]
-    ch_keep = jnp.where(core == 0, ch[:, :1], ch[:, 1:])
-    ch_send = jnp.where(core == 0, ch[:, 1:], ch[:, :1])
+    ch = ch_ref[...].astype(F32)
+    ch = jnp.concatenate([jnp.concatenate([ch[t], jnp.zeros((8 - ch.shape[1], ch.shape[2]), F32)], axis=0).T for t in range(ch.shape[0])], axis=0)
+    ch_keep = jnp.where(core == 0, ch[:, :1], ch[:, 1:2])
+    ch_send = jnp.where(core == 0, ch[:, 1:2], ch[:, :1])
     for e in range(experts):
         mask[0, e] = jnp.broadcast_to(jnp.where(ch_keep == e, 1.0, 0.0), (rows, LANES)).astype(BF16)
         mask[1, e] = jnp.broadcast_to(jnp.where(ch_send == e, 1.0, 0.0), (rows, LANES)).astype(BF16)
@@ -309,7 +317,7 @@
     total = part[own].astype(F32) + rs_in[0].astype(F32) + rs_in[1].astype(F32) + rs_in[2].astype(F32)
     x_new = (x_ref[...].astype(F32) + total).astype(BF16)
     x_mid[...] = x_new
-    h = normalise(x_new.astype(F32), g_ref[...].astype(F32), stat, stat_in, stat_sem, peers, width_full)
+    h = normalise(x_new.astype(F32), g_ref[...].astype(F32)[None, :], stat, stat_in, stat_sem, peers, width_full)
     h_own[...] = h
     sent = gather_y(h_own, h_all, ag_sem, yi, y_count, span)
     h_all[own] = h
@@ -320,7 +328,7 @@
     h2 = h_all[...]
     for e in range(experts):
         for s in range(2):
-            sparse[s, e] = h2 * wide_mask(s, e, width)
+            sparse[s, :, e * width:(e + 1) * width] = h2 * wide_mask(s, e, width)
 
     for copy in loads[:2 * experts]:
         copy.wait()
@@ -330,9 +338,7 @@
     first, second, to_cross, to_pair, forward = [], [], [], [], []
 
     def product(s, w, lo, n):
-        def body(e, acc):
-            return acc + dot(sparse[s, e], w[e, :, lo:lo + n])
-        return lax.fori_loop(0, experts, body, jnp.zeros((rows, n), F32))
+        return dot(sparse[s], w[:, lo:lo + n])
 
     def sums(k):
         lo, n = chunks[k]
@@ -352,7 +358,7 @@
         for c in lg:
             c.wait()
         logits = ((logit[...] + logit_in[0]) + (logit_in[1] + logit_in[2])).T[:rows]
-        col = lax.broadcasted_iota(jnp.int32, logits.shape, 1)
+        col = lax.broadcasted_iota(jnp.int32, logits.shape, 1).astype(F32)
         l_keep = jnp.sum(jnp.where(col == ch_keep, logits, 0.0), axis=1, keepdims=True)
         l_send = jnp.sum(jnp.where(col == ch_send, logits, 0.0), axis=1, keepdims=True)
         top = jnp.maximum(l_keep, l_send)
@@ -385,17 +391,24 @@
     sums(1)
     gates()
     sums(2)
-    unit(0)
     for k in range(3, n_chunk):
+        unit(k - 3)
         sums(k)
-    unit(1)
-    pass_on(0)
+        if k > 3:
+            pass_on(k - 4)
     for copy in loads[2 * experts:]:
         copy.wait()
-    for k in range(2, n_chunk):
-        unit(k)
-        pass_on(k - 1)
-        downward(k - 2)
+    unit(n_chunk - 3)
+    downward(0)
+    unit(n_chunk - 2)
+    downward(1)
+    pass_on(n_chunk - 4)
+    unit(n_chunk - 1)
+    pass_on(n_chunk - 3)
+    for k in range(2, n_chunk - 3):
+        downward(k)
+    pass_on(n_chunk - 2)
+    downward(n_chunk - 3)
     pass_on(n_chunk - 1)
     downward(n_chunk - 2)
     downward(n_chunk - 1)
@@ -420,14 +433,15 @@
     rows, heads = mixed.shape
     span, width = x_own.shape
     experts, _, ff = w_act.shape
-    half, chunks = rows // 2, chunks_of(ff, 384)
+    half, chunks = rows // 2, chunks_of(ff, 256)
     vmem, hbm = pl.BlockSpec(memory_space=pltpu.VMEM), pl.BlockSpec(memory_space=pl.ANY)
     down_t = jnp.transpose(w_down, (0, 2, 1))
     three = pltpu.SemaphoreType.DMA((2, 3))
     ring = pltpu.SemaphoreType.DMA((2, y_count - 1))
     per_chunk = pltpu.SemaphoreType.DMA((2, len(chunks)))
     buf = lambda lead, r, dt: [pltpu.VMEM(lead + (r, n), dt) for _, n in chunks]
-    scratch = [pltpu.VMEM(w_act.shape, BF16), pltpu.VMEM(w_act.shape, BF16), pltpu.VMEM(down_t.shape, BF16), pltpu.VMEM((8, LANES), F32), pltpu.VMEM((3, 8, LANES), F32), pltpu.VMEM((rows, width), BF16), pltpu.VMEM((y_count - 1, span, width), BF16), pltpu.VMEM((span, width), BF16), pltpu.VMEM((rows, width), BF16), pltpu.VMEM((experts, 2 * LANES), F32), pltpu.VMEM((3, experts, 2 * LANES), F32), pltpu.VMEM((rows, LANES), F32), pltpu.VMEM((2, experts, rows, LANES), BF16), pltpu.VMEM((2, experts, rows, width), BF16), pltpu.VMEM((rows, width), F32), pltpu.VMEM((span, width), BF16)]
+    flat = (experts * width, ff)
+    scratch = [pltpu.VMEM(flat, BF16), pltpu.VMEM(flat, BF16), pltpu.VMEM(down_t.shape, BF16), pltpu.VMEM((8, LANES), F32), pltpu.VMEM((3, 8, LANES), F32), pltpu.VMEM((rows, width), BF16), pltpu.VMEM((y_count - 1, span, width), BF16), pltpu.VMEM((span, width), BF16), pltpu.VMEM((rows, width), BF16), pltpu.VMEM((experts, 2 * LANES), F32), pltpu.VMEM((3, experts, 2 * LANES), F32), pltpu.VMEM((rows, LANES), F32), pltpu.VMEM((2, experts, rows, LANES), BF16), pltpu.VMEM((2, rows, experts * width), BF16), pltpu.VMEM((rows, width), F32), pltpu.VMEM((span, width), BF16)]
     scratch += buf((2,), rows, F32) + buf((2,), rows, BF16) + buf((2,), rows, BF16) + buf((2,), half, BF16) + buf((2,), half, BF16) + buf((), rows, BF16) + buf((), rows, BF16)
     scratch += [pltpu.SemaphoreType.DMA((3, experts)), three, ring, ring, three] + [per_chunk] * 5 + [ring, ring]
     return pl.pallas_call(
@@ -439,16 +453,15 @@
         compiler_params=pltpu.CompilerParams(collective_id=1, has_side_effects=True, vmem_limit_bytes=67043328),
         cost_estimate=pl.CostEstimate(flops=2 * 10 ** 10, bytes_accessed=6 * w_act.size, transcendentals=0),
         name="moe",
-    )(mixed, w_o, x_own, gain[None, :], w_router.T, choice, w_act, w_lin, down_t)
-
-
-def rope_tables(lengths, steps, heads, head):
+    )(mixed, w_o, x_own, gain, w_router.T, choice, w_act, w_lin, down_t)
+
+
+def rope_tables(lengths, steps, head):
     half = head // 2
     inv_freq = ROPE_BASE ** (-(jnp.arange(half, dtype=F32) * 2.0 / head))
     spots = (lengths[None, :] + jnp.arange(steps)[:, None]).reshape(-1).astype(F32)
     angles = spots[:, None] * inv_freq[None, :]
-    tile = lambda a: jnp.concatenate([a] * (2 * heads), axis=1)
-    return tile(jnp.cos(angles)), tile(jnp.sin(angles))
+    return jnp.cos(angles), jnp.sin(angles)
 
 
 def solution(mesh):
@@ -464,12 +477,11 @@
         rows = steps * n_batch
         width_full = emb_table.shape[1] * x_count
         span = rows // y_count
-        cos_t, sin_t = rope_tables(lengths, steps, heads, head)
-        own_tokens = lax.dynamic_slice(tokens.reshape(rows), (lax.axis_index('y') * span,), (span,))
-        x_own = gather(emb_table, own_tokens)
+        cos_t, sin_t = rope_tables(lengths, steps, head)
+        x_own = gather(emb_table, tokens, span)
         kvq = qkv_sums(x_own, g_attn, w_q, w_k, w_v, rows, y_count, width_full)
         mixed, k_out, v_out = attention(lengths, kvq, cos_t, sin_t, k_cache, v_cache, steps)
-        out = moe(mixed, w_o, x_own, g_ffn, w_router, choices.reshape(rows, 2), w_act, w_lin, w_down, y_count, width_full)
+        out = moe(mixed, w_o, x_own, g_ffn, w_router, jnp.transpose(choices, (0, 2, 1)), w_act, w_lin, w_down, y_count, width_full)
         return out.reshape(steps, n_batch, emb_table.shape[1]), k_out, v_out
 
     return jax.shard_map(per_device, mesh=mesh, in_specs=in_specs, out_specs=out_specs, check_vma=False)

time: 161 us -> 127 us (0.79)
  Pallas kernels: 148 us -> 123 us
  local copies, waits for them, and re-layouts: 10.1 us -> 1.74 us
    pallas_call x1, Pallas kernels: 91.4 us -> 66.2 us  [moe(): pl.pallas_call(functools.partial(moe_kernel, y_count, width_full, chunks,...]
    concatenate x2 -> x0, local copies, waits for them, and re-layouts: 2.63 us -> none  [rope_tables(): tile = lambda a: jnp.concatenate([a] * (2 * heads), axis=1)]
    broadcast_in_dim x4 -> x0, local copies, waits for them, and re-layouts: 1.95 us -> none  [the longest x2 0.78 us: gather(): tokens[:, None]]
where the time goes in v3:
time: 127 us
  Pallas kernels  123 us (97%)
  other arithmetic  1.77 us (1%)
  local copies, waits for them, and re-layouts  1.74 us (1%)
    pallas_call x1, Pallas kernels, moe(): pl.pallas_call(functools.partial(moe_kernel, y_count, width_full, chunks,...  66.2 us
    pallas_call x1, Pallas kernels, qkv_sums(): pl.pallas_call(functools.partial(qkv_kernel, y_count, width_full), in_spe...  28.5 us
    pallas_call x1, Pallas kernels, attention(): pl.pallas_call(functools.partial(attention_kernel, steps, batch, block, h...  19.1 us
    pallas_call x1, Pallas kernels, gather(): pl.pallas_call(functools.partial(gather_kernel, span, vocab, depth), grid...  9.03 us

profile of v3, /device:TPU:0, one launch (start us, length us, event | category | flops | bytes accessed | tf_op | source)
XLA Modules:
  0.0 127.0 jit_solution(3074982544355686312)
XLA Ops:
  0.6 0.7 add_convert_fusion
  1.3 0.1 convert_element_type.11
  1.4 9.0 %gather.1.x_ref = bf16[48,576]{1,0:T(8,128)(2,1)} custom-call(s32[3,64]{1,0:T(4,128)} %tok_ref.1, bf16[576,122753]{1,0:T(8,128)(2,1)} %bitcast.edge_ref.emb_ref, bf16[576,122753]{1,0:T(8,128)(2,1)} %bitcast.edge_ref.emb_ref), custom_call_target="tpu_custom_call" | custom-call | tf_op jit(solution)/shard_map/gather/pallas_call | solution.py:64
  10.4 1.1 multiply_sine_fusion
  11.5 28.5 %qkv_sums.1.kvq_ref = bf16[3,192,576]{2,1,0:T(8,128)(2,1)} custom-call(bf16[48,576]{1,0:T(8,128)(2,1)} %gather.1.x_ref, bf16[576]{0:T(1024)(128)(2,1)} %g_ref.2, bf16[576,576]{1,0:T(8,128)(2,1)} %wk_ref.1, bf16[576,576]{1,0:T(8,128)(2,1)} %wv_ref.1, bf16[576,576]{1,0:T(8,128)(2,1)} %wq_ref.1), custom_call_target="tpu_custom_call" | custom-call | flops 382205952 | bytes 2654208 | tf_op jit(solution)/shard_map/qkv_sums/pallas_call | solution.py:267
  40.1 19.1 %attention.1 = (bf16[192,576]{1,0:T(8,128)(2,1)}, bf16[64,9,64,128]{3,2,1,0:T(8,128)(2,1)}, bf16[64,9,64,128]{3,2,1,0:T(8,128)(2,1)}) custom-call(s32[64]{0:T(128)} %lens_ref.1, bf16[3,192,576]{2,1,0:T(8,128)(2,1)} %qkv_sums.1.kvq_ref, f32[192,32]{1,0:T(8,128)} %get-tuple-element.10.cos_ref, f32[192,32]{1,0:T(8,128)} %get-tuple-element.9.sin_ref, ...), custom_call_target="tpu_custom_call" | custom-call | flops 4000000000 | bytes 37748736 | tf_op jit(solution)/shard_map/attention/pallas_call | solution.py:154
  59.1 66.2 %moe.1 = bf16[192,576]{1,0:T(8,128)(2,1)} custom-call(bf16[192,576]{1,0:T(8,128)(2,1)} %get-tuple-element.6.o_ref, bf16[576,576]{1,0:T(8,128)(2,1)} %wo_ref.1, bf16[48,576]{1,0:T(8,128)(2,1)} %gather.1.x_ref, bf16[576]{0:T(1024)(128)(2,1)} %g_ref.3, bf16[8,576]{1,0:T(8,128)(2,1)} %bitcast.15, s32[3,2,64]{2,1,0:T(2,128)} %bitcast.16, ...), custom_call_target="tpu_custom_call" | custom-call | flops 20000000000 | bytes 39813120 | tf_op jit(solution)/shard_map/moe/pallas_call | solution.py:447
  125.3 1.7 %copy.21 = bf16[3,64,576]{2,1,0:T(8,128)(2,1)} copy(bf16[3,64,576]{2,1,0:T(8,128)(2,1)} %bitcast.11) | data formatting | bytes 442368
  (1 shorter events, 0.0 us)

commit v4 on v3

--- a/solution.py
+++ b/solution.py
@@ -130,12 +130,12 @@
     scores = jnp.concatenate(scores_all, axis=0)
     peak = jnp.max(scores, axis=-1, keepdims=True)
     weight = jnp.exp(scores - peak)
-    total = jnp.sum(weight, axis=-1, keepdims=True)
+    inverse = 1.0 / jnp.sum(weight, axis=-1, keepdims=True)
     weight = weight.astype(BF16)
     span = steps * hpad
     for n in range(block):
         b = i * block + n
-        mixed = dot_nt(weight[n * span:(n + 1) * span], news[n]) / total[n * span:(n + 1) * span]
+        mixed = dot_nt(weight[n * span:(n + 1) * span], news[n]) * inverse[n * span:(n + 1) * span]
         for t in range(steps):
             o_rows[t, pl.ds(b, 1), :] = jnp.sum(jnp.where(head_mask, mixed[t * hpad:(t + 1) * hpad], 0.0), axis=0, keepdims=True)
 
@@ -179,13 +179,13 @@
     return xi, yi, core, chip, pair, cross, diag
 
 
-def enter(x_peers, yi, y_count):
+def knock(x_peers, yi, y_count):
     barrier = pltpu.get_barrier_semaphore()
     for peer in x_peers:
         pl.semaphore_signal(barrier, inc=1, device_id={X: peer}, device_id_type=MESH)
     for d in range(1, y_count):
         pl.semaphore_signal(barrier, inc=1, device_id={Y: lax.rem(yi + d, y_count)}, device_id_type=MESH)
-    pl.semaphore_wait(barrier, len(x_peers) + y_count - 1)
+    return lambda: pl.semaphore_wait(barrier, len(x_peers) + y_count - 1)
 
 
 def remote(src, dst, send, recv, **where):
@@ -212,10 +212,12 @@
     return start_all([remote(src, dst.at[rows], sems.at[0, d - 1], sems.at[1, d - 1], y=lax.rem(yi + d, y_count)) for d in range(1, y_count)])
 
 
-def normalise(x_f32, gain, stat, stat_in, sems, peers, width_full):
+def normalise(x_f32, gain, stat, stat_in, sems, peers, width_full, ready=None):
     rows = x_f32.shape[0]
     part = jnp.sum(x_f32 * x_f32, axis=-1, keepdims=True)
     stat[:, :rows] = jnp.broadcast_to(part, (rows, LANES)).T[:8]
+    if ready:
+        ready()
     copies = start_all([remote(stat, stat_in.at[i], sems.at[0, i], sems.at[1, i], x=peer) for i, peer in enumerate(peers)])
     for c in copies:
         c.wait()
@@ -223,13 +225,14 @@
     return (x_f32 * lax.rsqrt(total / width_full + EPS) * gain).astype(BF16)
 
 
-def qkv_kernel(y_count, width_full, x_ref, g_ref, wk_ref, wv_ref, wq_ref, out_ref, stat, stat_in, h_own, h_all, keep, snd1, rcv1, snd2, rcv2, done, rcv3, stat_sem, y_sem, s1, s2, s3):
+def qkv_kernel(y_count, width_full, x_ref, g_ref, wk_hbm, wv_hbm, wq_hbm, out_ref, weights, w_sem, stat, stat_in, h_own, h_all, keep, snd1, rcv1, snd2, rcv2, done, rcv3, stat_sem, y_sem, s1, s2, s3):
     xi, yi, core, chip, pair, cross, diag = positions()
     span, rows = x_ref.shape[0], h_all.shape[0]
     half = rows // 2
+    ready = knock((pair, cross, diag), yi, y_count)
+    loads = start_all([pltpu.make_async_copy(w, weights.at[m], w_sem.at[m]) for m, w in enumerate((wk_hbm, wv_hbm, wq_hbm))])
     stat[...] = jnp.zeros_like(stat)
-    enter((pair, cross, diag), yi, y_count)
-    h = normalise(x_ref[...].astype(F32), g_ref[...].astype(F32)[None, :], stat, stat_in, stat_sem, (pair, cross, diag), width_full)
+    h = normalise(x_ref[...].astype(F32), g_ref[...].astype(F32)[None, :], stat, stat_in, stat_sem, (pair, cross, diag), width_full, ready)
     h_own[...] = h
     sent = gather_y(h_own, h_all, y_sem, yi, y_count, span)
     h_all[pl.ds(pl.multiple_of(yi * span, span), span)] = h
@@ -238,11 +241,11 @@
     mine = pl.ds(pl.multiple_of(core * half, half), half)
     theirs = pl.ds(pl.multiple_of((1 - core) * half, half), half)
     first, second, third = [], [], []
-    weights = (wk_ref, wv_ref, wq_ref)
     for m in range(3):
-        snd1[m] = dot(h_all[theirs], weights[m][...]).astype(BF16)
+        loads[m].wait()
+        snd1[m] = dot(h_all[theirs], weights[m]).astype(BF16)
         first += start_all([remote(snd1.at[m], rcv1.at[m], s1.at[0, m], s1.at[1, m], x=pair)])
-        keep[m] = dot(h_all[mine], weights[m][...])
+        keep[m] = dot(h_all[mine], weights[m])
         first[m].wait_recv()
         snd2[m] = (keep[m] + rcv1[m].astype(F32)).astype(BF16)
         second += start_all([remote(snd2.at[m], rcv2.at[m], s2.at[0, m], s2.at[1, m], x=cross)])
@@ -266,10 +269,10 @@
     pairs = pltpu.SemaphoreType.DMA((2, 3))
     return pl.pallas_call(
         functools.partial(qkv_kernel, y_count, width_full),
-        in_specs=[vmem] * 5,
+        in_specs=[vmem] * 2 + [pl.BlockSpec(memory_space=pl.ANY)] * 3,
         out_specs=vmem,
         out_shape=jax.ShapeDtypeStruct((3, rows, cols), BF16),
-        scratch_shapes=[pltpu.VMEM((8, LANES), F32), pltpu.VMEM((3, 8, LANES), F32), pltpu.VMEM((span, width), BF16), pltpu.VMEM((rows, width), BF16), pltpu.VMEM((3, half, cols), F32), part, part, part, part, part, part, pairs, pltpu.SemaphoreType.DMA((2, y_count - 1)), pairs, pairs, pairs],
+        scratch_shapes=[pltpu.VMEM((3, width, cols), BF16), pltpu.SemaphoreType.DMA((3,)), pltpu.VMEM((8, LANES), F32), pltpu.VMEM((3, 8, LANES), F32), pltpu.VMEM((span, width), BF16), pltpu.VMEM((rows, width), BF16), pltpu.VMEM((3, half, cols), F32), part, part, part, part, part, part, pairs, pltpu.SemaphoreType.DMA((2, y_count - 1)), pairs, pairs, pairs],
         compiler_params=pltpu.CompilerParams(collective_id=0, has_side_effects=True),
         cost_estimate=pl.CostEstimate(flops=6 * rows * width * cols, bytes_accessed=8 * width * cols, transcendentals=0),
         name="qkv_sums",
@@ -280,14 +283,19 @@
     return tuple((lo, min(wide, ff - lo)) for lo in range(0, ff, wide))
 
 
-def moe_kernel(y_count, width_full, chunks, experts, o_ref, wo_ref, x_ref, g_ref, wr_ref, ch_ref, act_hbm, lin_hbm, down_hbm, out_ref, act, lin, down, stat, stat_in, part, rs_in, h_own, h_all, logit, logit_in, gate, mask, sparse, acc_down, x_mid, *rest):
+def moe_kernel(y_count, width_full, chunks, halves, experts, o_ref, wo_hbm, x_ref, g_ref, wr_ref, ch_ref, act_hbm, lin_hbm, down_hbm, out_ref, act, lin, down, stat, stat_in, part, rs_in, h_own, h_all, logit, logit_in, gate, mask, sparse, acc_down, x_mid, wo, wo_sem, *rest):
     n_chunk = len(chunks)
     keep, snd1, rcv1, snd2, rcv2, u_mine, u_pair = [rest[i * n_chunk:(i + 1) * n_chunk] for i in range(7)]
-    w_sem, stat_sem, rs_sem, ag_sem, lg_sem, s1, s2, s3, s4, s5, rs2_sem, ag2_sem = rest[7 * n_chunk:]
+    last = rest[7 * n_chunk:7 * n_chunk + 8]
+    part2, rs2_in, own2, all2 = last[:2], last[2:4], last[4:6], last[6:]
+    w_sem, stat_sem, rs_sem, ag_sem, lg_sem, s1, s2, s3, s4, s5, rs2_sem, ag2_sem = rest[7 * n_chunk + 8:]
     xi, yi, core, chip, pair, cross, diag = positions()
     peers = (pair, cross, diag)
     span, rows = x_ref.shape[0], h_all.shape[0]
     half, width = rows // 2, x_ref.shape[1]
+    ready = knock(peers, yi, y_count)
+    wo_load = pltpu.make_async_copy(wo_hbm, wo, wo_sem)
+    wo_load.start()
     loads = []
     for i, (src, dst) in enumerate(((act_hbm, act), (lin_hbm, lin), (down_hbm, down))):
         for e in range(experts):
@@ -296,11 +304,9 @@
     start_all(loads)
     stat[...] = jnp.zeros_like(stat)
     logit[...] = jnp.zeros_like(logit)
-    enter(peers, yi, y_count)
-
     own = pl.ds(pl.multiple_of(yi * span, span), span)
-    part[...] = dot(o_ref[...], wo_ref[...]).astype(BF16)
-    sent = scatter_y(part, rs_in, rs_sem, yi, y_count, span)
+    wo_load.wait()
+    part[...] = dot(o_ref[...], wo[...]).astype(BF16)
     ch = ch_ref[...].astype(F32)
     ch = jnp.concatenate([jnp.concatenate([ch[t], jnp.zeros((8 - ch.shape[1], ch.shape[2]), F32)], axis=0).T for t in range(ch.shape[0])], axis=0)
     ch_keep = jnp.where(core == 0, ch[:, :1], ch[:, 1:2])
@@ -308,6 +314,9 @@
     for e in range(experts):
         mask[0, e] = jnp.broadcast_to(jnp.where(ch_keep == e, 1.0, 0.0), (rows, LANES)).astype(BF16)
         mask[1, e] = jnp.broadcast_to(jnp.where(ch_send == e, 1.0, 0.0), (rows, LANES)).astype(BF16)
+
+    ready()
+    sent = scatter_y(part, rs_in, rs_sem, yi, y_count, span)
 
     def wide_mask(s, e, n):
         return jnp.concatenate([mask[s, e]] * (n // LANES) + ([mask[s, e][:, :n % LANES]] if n % LANES else []), axis=1)
@@ -382,9 +391,9 @@
         to_pair[k].wait_recv()
         forward[k].wait_recv()
         u0, u1 = u_mine[k][...], u_pair[k][...]
-        total = jnp.zeros((rows, width), F32) if k == 0 else acc_down[...]
+        total = jnp.zeros((width, rows), F32) if k == 0 else acc_down[...]
         for e in range(experts):
-            total = total + dot_nt(u0 * wide_mask(0, e, n) + u1 * wide_mask(1, e, n), down[e, :, lo:lo + n])
+            total = total + dot_nt(down[e, :, lo:lo + n], u0 * wide_mask(0, e, n) + u1 * wide_mask(1, e, n))
         acc_down[...] = total
 
     sums(0)
@@ -413,18 +422,22 @@
     downward(n_chunk - 2)
     downward(n_chunk - 1)
 
-    part[...] = acc_down[...].astype(BF16)
-    sent = scatter_y(part, rs_in, rs2_sem, yi, y_count, span)
-    for c in sent:
-        c.wait()
-    total = part[own].astype(F32) + rs_in[0].astype(F32) + rs_in[1].astype(F32) + rs_in[2].astype(F32)
-    h_new = (x_mid[...].astype(F32) + total).astype(BF16)
-    h_own[...] = h_new
-    sent = gather_y(h_own, h_all, ag2_sem, yi, y_count, span)
-    h_all[own] = h_new
-    for c in sent:
-        c.wait()
-    out_ref[...] = h_all[...]
+    sums2, copies2 = [], []
+    for i, (lo, n) in enumerate(halves):
+        part2[i][...] = acc_down[lo:lo + n].T.astype(BF16)
+        sums2.append(scatter_y(part2[i], rs2_in[i], rs2_sem.at[i], yi, y_count, span))
+    for i, (lo, n) in enumerate(halves):
+        for c in sums2[i]:
+            c.wait()
+        total = part2[i][own].astype(F32) + rs2_in[i][0].astype(F32) + rs2_in[i][1].astype(F32) + rs2_in[i][2].astype(F32)
+        h_new = (x_mid[:, lo:lo + n].astype(F32) + total).astype(BF16)
+        own2[i][...] = h_new
+        copies2.append(gather_y(own2[i], all2[i], ag2_sem.at[i], yi, y_count, span))
+        all2[i][own] = h_new
+    for i, (lo, n) in enumerate(halves):
+        for c in copies2[i]:
+            c.wait()
+        out_ref[:, lo:lo + n] = all2[i][...]
     for c in first + second + to_cross + to_pair + forward:
         c.wait_send()
 
@@ -434,6 +447,7 @@
     span, width = x_own.shape
     experts, _, ff = w_act.shape
     half, chunks = rows // 2, chunks_of(ff, 256)
+    halves = ((0, 256), (256, width - 256))
     vmem, hbm = pl.BlockSpec(memory_space=pltpu.VMEM), pl.BlockSpec(memory_space=pl.ANY)
     down_t = jnp.transpose(w_down, (0, 2, 1))
     three = pltpu.SemaphoreType.DMA((2, 3))
@@ -441,12 +455,15 @@
     per_chunk = pltpu.SemaphoreType.DMA((2, len(chunks)))
     buf = lambda lead, r, dt: [pltpu.VMEM(lead + (r, n), dt) for _, n in chunks]
     flat = (experts * width, ff)
-    scratch = [pltpu.VMEM(flat, BF16), pltpu.VMEM(flat, BF16), pltpu.VMEM(down_t.shape, BF16), pltpu.VMEM((8, LANES), F32), pltpu.VMEM((3, 8, LANES), F32), pltpu.VMEM((rows, width), BF16), pltpu.VMEM((y_count - 1, span, width), BF16), pltpu.VMEM((span, width), BF16), pltpu.VMEM((rows, width), BF16), pltpu.VMEM((experts, 2 * LANES), F32), pltpu.VMEM((3, experts, 2 * LANES), F32), pltpu.VMEM((rows, LANES), F32), pltpu.VMEM((2, experts, rows, LANES), BF16), pltpu.VMEM((2, rows, experts * width), BF16), pltpu.VMEM((rows, width), F32), pltpu.VMEM((span, width), BF16)]
+    scratch = [pltpu.VMEM(flat, BF16), pltpu.VMEM(flat, BF16), pltpu.VMEM(down_t.shape, BF16), pltpu.VMEM((8, LANES), F32), pltpu.VMEM((3, 8, LANES), F32), pltpu.VMEM((rows, width), BF16), pltpu.VMEM((y_count - 1, span, width), BF16), pltpu.VMEM((span, width), BF16), pltpu.VMEM((rows, width), BF16), pltpu.VMEM((experts, 2 * LANES), F32), pltpu.VMEM((3, experts, 2 * LANES), F32), pltpu.VMEM((rows, LANES), F32), pltpu.VMEM((2, experts, rows, LANES), BF16), pltpu.VMEM((2, rows, experts * width), BF16), pltpu.VMEM((width, rows), F32), pltpu.VMEM((span, width), BF16), pltpu.VMEM(w_o.shape, BF16), pltpu.SemaphoreType.DMA]
     scratch += buf((2,), rows, F32) + buf((2,), rows, BF16) + buf((2,), rows, BF16) + buf((2,), half, BF16) + buf((2,), half, BF16) + buf((), rows, BF16) + buf((), rows, BF16)
-    scratch += [pltpu.SemaphoreType.DMA((3, experts)), three, ring, ring, three] + [per_chunk] * 5 + [ring, ring]
+    for lead, r in (((), rows), ((y_count - 1,), span), ((), span), ((), rows)):
+        scratch += [pltpu.VMEM(lead + (r, n), BF16) for _, n in halves]
+    rings = pltpu.SemaphoreType.DMA((2, 2, y_count - 1))
+    scratch += [pltpu.SemaphoreType.DMA((3, experts)), three, ring, ring, three] + [per_chunk] * 5 + [rings, rings]
     return pl.pallas_call(
-        functools.partial(moe_kernel, y_count, width_full, chunks, experts),
-        in_specs=[vmem] * 6 + [hbm] * 3,
+        functools.partial(moe_kernel, y_count, width_full, chunks, halves, experts),
+        in_specs=[vmem, hbm] + [vmem] * 4 + [hbm] * 3,
         out_specs=vmem,
         out_shape=jax.ShapeDtypeStruct((rows, width), BF16),
         scratch_shapes=scratch,

time: 127 us -> 137 us (1.079)
  Pallas kernels: 123 us -> 133 us
    pallas_call x1, Pallas kernels: 66.2 us -> 76.9 us  [moe(): pl.pallas_call(functools.partial(moe_kernel, y_count, width_full, chunks,...]
where the time goes in v4:
time: 137 us
  Pallas kernels  133 us (97%)
  other arithmetic  1.77 us (1%)
  local copies, waits for them, and re-layouts  1.74 us (1%)
    pallas_call x1, Pallas kernels, moe(): pl.pallas_call(functools.partial(moe_kernel, y_count, width_full, chunks,...  76.9 us
    pallas_call x1, Pallas kernels, qkv_sums(): pl.pallas_call(functools.partial(qkv_kernel, y_count, width_full), in_spe...  27.6 us
    pallas_call x1, Pallas kernels, attention(): pl.pallas_call(functools.partial(attention_kernel, steps, batch, block, h...  19.1 us
    pallas_call x1, Pallas kernels, gather(): pl.pallas_call(functools.partial(gather_kernel, span, vocab, depth), grid...  9.03 us

profile of v4, /device:TPU:0, one launch (start us, length us, event | category | flops | bytes accessed | tf_op | source)
XLA Modules:
  0.0 136.8 jit_solution(14350714155325043969)
XLA Ops:
  0.6 0.7 add_convert_fusion
  1.3 0.1 convert_element_type.11
  1.4 9.0 %gather.1.x_ref = bf16[48,576]{1,0:T(8,128)(2,1)} custom-call(s32[3,64]{1,0:T(4,128)} %tok_ref.1, bf16[576,122753]{1,0:T(8,128)(2,1)} %bitcast.edge_ref.emb_ref, bf16[576,122753]{1,0:T(8,128)(2,1)} %bitcast.edge_ref.emb_ref), custom_call_target="tpu_custom_call" | custom-call | tf_op jit(solution)/shard_map/gather/pallas_call | solution.py:64
  10.4 1.1 multiply_sine_fusion
  11.5 27.6 %qkv_sums.1.kvq_ref = bf16[3,192,576]{2,1,0:T(8,128)(2,1)} custom-call(bf16[48,576]{1,0:T(8,128)(2,1)} %gather.1.x_ref, bf16[576]{0:T(1024)(128)(2,1)} %g_ref.2, bf16[576,576]{1,0:T(8,128)(2,1)} %wk_hbm.1, bf16[576,576]{1,0:T(8,128)(2,1)} %wv_hbm.1, bf16[576,576]{1,0:T(8,128)(2,1)} %wq_hbm.1), custom_call_target="tpu_custom_call" | custom-call | flops 382205952 | bytes 2654208 | tf_op jit(solution)/shard_map/qkv_sums/pallas_call | solution.py:270
  39.2 19.1 %attention.1 = (bf16[192,576]{1,0:T(8,128)(2,1)}, bf16[64,9,64,128]{3,2,1,0:T(8,128)(2,1)}, bf16[64,9,64,128]{3,2,1,0:T(8,128)(2,1)}) custom-call(s32[64]{0:T(128)} %lens_ref.1, bf16[3,192,576]{2,1,0:T(8,128)(2,1)} %qkv_sums.1.kvq_ref, f32[192,32]{1,0:T(8,128)} %get-tuple-element.10.cos_ref, f32[192,32]{1,0:T(8,128)} %get-tuple-element.9.sin_ref, ...), custom_call_target="tpu_custom_call" | custom-call | flops 4000000000 | bytes 37748736 | tf_op jit(solution)/shard_map/attention/pallas_call | solution.py:154
  58.2 76.9 %moe.1 = bf16[192,576]{1,0:T(8,128)(2,1)} custom-call(bf16[192,576]{1,0:T(8,128)(2,1)} %get-tuple-element.6.o_ref, bf16[576,576]{1,0:T(8,128)(2,1)} %wo_hbm.1, bf16[48,576]{1,0:T(8,128)(2,1)} %gather.1.x_ref, bf16[576]{0:T(1024)(128)(2,1)} %g_ref.3, bf16[8,576]{1,0:T(8,128)(2,1)} %bitcast.15, s32[3,2,64]{2,1,0:T(2,128)} %bitcast.16, ...), custom_call_target="tpu_custom_call" | custom-call | flops 20000000000 | bytes 39813120 | tf_op jit(solution)/shard_map/moe/pallas_call | solution.py:464
  135.1 1.7 %copy.21 = bf16[3,64,576]{2,1,0:T(8,128)(2,1)} copy(bf16[3,64,576]{2,1,0:T(8,128)(2,1)} %bitcast.11) | data formatting | bytes 442368
  (1 shorter events, 0.0 us)

commit v5 on v4

--- a/solution.py
+++ b/solution.py
@@ -391,9 +391,9 @@
         to_pair[k].wait_recv()
         forward[k].wait_recv()
         u0, u1 = u_mine[k][...], u_pair[k][...]
-        total = jnp.zeros((width, rows), F32) if k == 0 else acc_down[...]
+        total = jnp.zeros((rows, width), F32) if k == 0 else acc_down[...]
         for e in range(experts):
-            total = total + dot_nt(down[e, :, lo:lo + n], u0 * wide_mask(0, e, n) + u1 * wide_mask(1, e, n))
+            total = total + dot_nt(u0 * wide_mask(0, e, n) + u1 * wide_mask(1, e, n), down[e, :, lo:lo + n])
         acc_down[...] = total
 
     sums(0)
@@ -410,21 +410,20 @@
     unit(n_chunk - 3)
     downward(0)
     unit(n_chunk - 2)
-    downward(1)
     pass_on(n_chunk - 4)
+    for k in range(1, n_chunk - 3):
+        downward(k)
     unit(n_chunk - 1)
     pass_on(n_chunk - 3)
-    for k in range(2, n_chunk - 3):
-        downward(k)
+    downward(n_chunk - 3)
     pass_on(n_chunk - 2)
-    downward(n_chunk - 3)
+    downward(n_chunk - 2)
     pass_on(n_chunk - 1)
-    downward(n_chunk - 2)
     downward(n_chunk - 1)
 
     sums2, copies2 = [], []
     for i, (lo, n) in enumerate(halves):
-        part2[i][...] = acc_down[lo:lo + n].T.astype(BF16)
+        part2[i][...] = acc_down[:, lo:lo + n].astype(BF16)
         sums2.append(scatter_y(part2[i], rs2_in[i], rs2_sem.at[i], yi, y_count, span))
     for i, (lo, n) in enumerate(halves):
         for c in sums2[i]:
@@ -455,7 +454,7 @@
     per_chunk = pltpu.SemaphoreType.DMA((2, len(chunks)))
     buf = lambda lead, r, dt: [pltpu.VMEM(lead + (r, n), dt) for _, n in chunks]
     flat = (experts * width, ff)
-    scratch = [pltpu.VMEM(flat, BF16), pltpu.VMEM(flat, BF16), pltpu.VMEM(down_t.shape, BF16), pltpu.VMEM((8, LANES), F32), pltpu.VMEM((3, 8, LANES), F32), pltpu.VMEM((rows, width), BF16), pltpu.VMEM((y_count - 1, span, width), BF16), pltpu.VMEM((span, width), BF16), pltpu.VMEM((rows, width), BF16), pltpu.VMEM((experts, 2 * LANES), F32), pltpu.VMEM((3, experts, 2 * LANES), F32), pltpu.VMEM((rows, LANES), F32), pltpu.VMEM((2, experts, rows, LANES), BF16), pltpu.VMEM((2, rows, experts * width), BF16), pltpu.VMEM((width, rows), F32), pltpu.VMEM((span, width), BF16), pltpu.VMEM(w_o.shape, BF16), pltpu.SemaphoreType.DMA]
+    scratch = [pltpu.VMEM(flat, BF16), pltpu.VMEM(flat, BF16), pltpu.VMEM(down_t.shape, BF16), pltpu.VMEM((8, LANES), F32), pltpu.VMEM((3, 8, LANES), F32), pltpu.VMEM((rows, width), BF16), pltpu.VMEM((y_count - 1, span, width), BF16), pltpu.VMEM((span, width), BF16), pltpu.VMEM((rows, width), BF16), pltpu.VMEM((experts, 2 * LANES), F32), pltpu.VMEM((3, experts, 2 * LANES), F32), pltpu.VMEM((rows, LANES), F32), pltpu.VMEM((2, experts, rows, LANES), BF16), pltpu.VMEM((2, rows, experts * width), BF16), pltpu.VMEM((rows, width), F32), pltpu.VMEM((span, width), BF16), pltpu.VMEM(w_o.shape, BF16), pltpu.SemaphoreType.DMA]
     scratch += buf((2,), rows, F32) + buf((2,), rows, BF16) + buf((2,), rows, BF16) + buf((2,), half, BF16) + buf((2,), half, BF16) + buf((), rows, BF16) + buf((), rows, BF16)
     for lead, r in (((), rows), ((y_count - 1,), span), ((), span), ((), rows)):
         scratch += [pltpu.VMEM(lead + (r, n), BF16) for _, n in halves]

time: 137 us -> 139 us (1.015)
  Pallas kernels: 133 us -> 135 us
    pallas_call x1, Pallas kernels: 76.9 us -> 78.8 us  [moe(): pl.pallas_call(functools.partial(moe_kernel, y_count, width_full, chunks,...]
where the time goes in v5:
time: 139 us
  Pallas kernels  135 us (97%)
  other arithmetic  1.77 us (1%)
  local copies, waits for them, and re-layouts  1.74 us (1%)
    pallas_call x1, Pallas kernels, moe(): pl.pallas_call(functools.partial(moe_kernel, y_count, width_full, chunks,...  78.8 us
    pallas_call x1, Pallas kernels, qkv_sums(): pl.pallas_call(functools.partial(qkv_kernel, y_count, width_full), in_spe...  27.6 us
    pallas_call x1, Pallas kernels, attention(): pl.pallas_call(functools.partial(attention_kernel, steps, batch, block, h...  19.1 us
    pallas_call x1, Pallas kernels, gather(): pl.pallas_call(functools.partial(gather_kernel, span, vocab, depth), grid...  9.03 us

profile of v5, /device:TPU:0, one launch (start us, length us, event | category | flops | bytes accessed | tf_op | source)
XLA Modules:
  0.0 138.7 jit_solution(17521196405899382029)
XLA Ops:
  0.6 0.7 add_convert_fusion
  1.3 0.1 convert_element_type.11
  1.4 9.0 %gather.1.x_ref = bf16[48,576]{1,0:T(8,128)(2,1)} custom-call(s32[3,64]{1,0:T(4,128)} %tok_ref.1, bf16[576,122753]{1,0:T(8,128)(2,1)} %bitcast.edge_ref.emb_ref, bf16[576,122753]{1,0:T(8,128)(2,1)} %bitcast.edge_ref.emb_ref), custom_call_target="tpu_custom_call" | custom-call | tf_op jit(solution)/shard_map/gather/pallas_call | solution.py:64
  10.4 1.1 multiply_sine_fusion
  11.5 27.6 %qkv_sums.1.kvq_ref = bf16[3,192,576]{2,1,0:T(8,128)(2,1)} custom-call(bf16[48,576]{1,0:T(8,128)(2,1)} %gather.1.x_ref, bf16[576]{0:T(1024)(128)(2,1)} %g_ref.2, bf16[576,576]{1,0:T(8,128)(2,1)} %wk_hbm.1, bf16[576,576]{1,0:T(8,128)(2,1)} %wv_hbm.1, bf16[576,576]{1,0:T(8,128)(2,1)} %wq_hbm.1), custom_call_target="tpu_custom_call" | custom-call | flops 382205952 | bytes 2654208 | tf_op jit(solution)/shard_map/qkv_sums/pallas_call | solution.py:270
  39.2 19.1 %attention.1 = (bf16[192,576]{1,0:T(8,128)(2,1)}, bf16[64,9,64,128]{3,2,1,0:T(8,128)(2,1)}, bf16[64,9,64,128]{3,2,1,0:T(8,128)(2,1)}) custom-call(s32[64]{0:T(128)} %lens_ref.1, bf16[3,192,576]{2,1,0:T(8,128)(2,1)} %qkv_sums.1.kvq_ref, f32[192,32]{1,0:T(8,128)} %get-tuple-element.10.cos_ref, f32[192,32]{1,0:T(8,128)} %get-tuple-element.9.sin_ref, ...), custom_call_target="tpu_custom_call" | custom-call | flops 4000000000 | bytes 37748736 | tf_op jit(solution)/shard_map/attention/pallas_call | solution.py:154
  58.2 78.8 %moe.1 = bf16[192,576]{1,0:T(8,128)(2,1)} custom-call(bf16[192,576]{1,0:T(8,128)(2,1)} %get-tuple-element.6.o_ref, bf16[576,576]{1,0:T(8,128)(2,1)} %wo_hbm.1, bf16[48,576]{1,0:T(8,128)(2,1)} %gather.1.x_ref, bf16[576]{0:T(1024)(128)(2,1)} %g_ref.3, bf16[8,576]{1,0:T(8,128)(2,1)} %bitcast.15, s32[3,2,64]{2,1,0:T(2,128)} %bitcast.16, ...), custom_call_target="tpu_custom_call" | custom-call | flops 20000000000 | bytes 39813120 | tf_op jit(solution)/shard_map/moe/pallas_call | solution.py:463
  137.0 1.7 %copy.21 = bf16[3,64,576]{2,1,0:T(8,128)(2,1)} copy(bf16[3,64,576]{2,1,0:T(8,128)(2,1)} %bitcast.11) | data formatting | bytes 442368
  (1 shorter events, 0.0 us)

commit v6 on v5

--- a/solution.py
+++ b/solution.py
@@ -301,11 +301,11 @@
         for e in range(experts):
             place = dst.at[e] if i == 2 else dst.at[pl.ds(e * width, width)]
             loads.append(pltpu.make_async_copy(src.at[e], place, w_sem.at[i, e]))
-    start_all(loads)
     stat[...] = jnp.zeros_like(stat)
     logit[...] = jnp.zeros_like(logit)
     own = pl.ds(pl.multiple_of(yi * span, span), span)
     wo_load.wait()
+    start_all(loads)
     part[...] = dot(o_ref[...], wo[...]).astype(BF16)
     ch = ch_ref[...].astype(F32)
     ch = jnp.concatenate([jnp.concatenate([ch[t], jnp.zeros((8 - ch.shape[1], ch.shape[2]), F32)], axis=0).T for t in range(ch.shape[0])], axis=0)
@@ -391,9 +391,9 @@
         to_pair[k].wait_recv()
         forward[k].wait_recv()
         u0, u1 = u_mine[k][...], u_pair[k][...]
-        total = jnp.zeros((rows, width), F32) if k == 0 else acc_down[...]
+        total = jnp.zeros((width, rows), F32) if k == 0 else acc_down[...]
         for e in range(experts):
-            total = total + dot_nt(u0 * wide_mask(0, e, n) + u1 * wide_mask(1, e, n), down[e, :, lo:lo + n])
+            total = total + dot_nt(down[e, :, lo:lo + n], u0 * wide_mask(0, e, n) + u1 * wide_mask(1, e, n))
         acc_down[...] = total
 
     sums(0)
@@ -423,7 +423,7 @@
 
     sums2, copies2 = [], []
     for i, (lo, n) in enumerate(halves):
-        part2[i][...] = acc_down[:, lo:lo + n].astype(BF16)
+        part2[i][...] = acc_down[lo:lo + n].T.astype(BF16)
         sums2.append(scatter_y(part2[i], rs2_in[i], rs2_sem.at[i], yi, y_count, span))
     for i, (lo, n) in enumerate(halves):
         for c in sums2[i]:
@@ -454,7 +454,7 @@
     per_chunk = pltpu.SemaphoreType.DMA((2, len(chunks)))
     buf = lambda lead, r, dt: [pltpu.VMEM(lead + (r, n), dt) for _, n in chunks]
     flat = (experts * width, ff)
-    scratch = [pltpu.VMEM(flat, BF16), pltpu.VMEM(flat, BF16), pltpu.VMEM(down_t.shape, BF16), pltpu.VMEM((8, LANES), F32), pltpu.VMEM((3, 8, LANES), F32), pltpu.VMEM((rows, width), BF16), pltpu.VMEM((y_count - 1, span, width), BF16), pltpu.VMEM((span, width), BF16), pltpu.VMEM((rows, width), BF16), pltpu.VMEM((experts, 2 * LANES), F32), pltpu.VMEM((3, experts, 2 * LANES), F32), pltpu.VMEM((rows, LANES), F32), pltpu.VMEM((2, experts, rows, LANES), BF16), pltpu.VMEM((2, rows, experts * width), BF16), pltpu.VMEM((rows, width), F32), pltpu.VMEM((span, width), BF16), pltpu.VMEM(w_o.shape, BF16), pltpu.SemaphoreType.DMA]
+    scratch = [pltpu.VMEM(flat, BF16), pltpu.VMEM(flat, BF16), pltpu.VMEM(down_t.shape, BF16), pltpu.VMEM((8, LANES), F32), pltpu.VMEM((3, 8, LANES), F32), pltpu.VMEM((rows, width), BF16), pltpu.VMEM((y_count - 1, span, width), BF16), pltpu.VMEM((span, width), BF16), pltpu.VMEM((rows, width), BF16), pltpu.VMEM((experts, 2 * LANES), F32), pltpu.VMEM((3, experts, 2 * LANES), F32), pltpu.VMEM((rows, LANES), F32), pltpu.VMEM((2, experts, rows, LANES), BF16), pltpu.VMEM((2, rows, experts * width), BF16), pltpu.VMEM((width, rows), F32), pltpu.VMEM((span, width), BF16), pltpu.VMEM(w_o.shape, BF16), pltpu.SemaphoreType.DMA]
     scratch += buf((2,), rows, F32) + buf((2,), rows, BF16) + buf((2,), rows, BF16) + buf((2,), half, BF16) + buf((2,), half, BF16) + buf((), rows, BF16) + buf((), rows, BF16)
     for lead, r in (((), rows), ((y_count - 1,), span), ((), span), ((), rows)):
         scratch += [pltpu.VMEM(lead + (r, n), BF16) for _, n in halves]

time: 139 us -> 126 us (0.906)
  Pallas kernels: 135 us -> 122 us
    pallas_call x1, Pallas kernels: 78.8 us -> 66 us  [moe(): pl.pallas_call(functools.partial(moe_kernel, y_count, width_full, chunks,...]
where the time goes in v6:
time: 126 us
  Pallas kernels  122 us (97%)
  other arithmetic  1.77 us (1%)
  local copies, waits for them, and re-layouts  1.74 us (1%)
    pallas_call x1, Pallas kernels, moe(): pl.pallas_call(functools.partial(moe_kernel, y_count, width_full, chunks,...  66 us
    pallas_call x1, Pallas kernels, qkv_sums(): pl.pallas_call(functools.partial(qkv_kernel, y_count, width_full), in_spe...  27.6 us
    pallas_call x1, Pallas kernels, attention(): pl.pallas_call(functools.partial(attention_kernel, steps, batch, block, h...  19.1 us
    pallas_call x1, Pallas kernels, gather(): pl.pallas_call(functools.partial(gather_kernel, span, vocab, depth), grid...  9.03 us

profile of v6, /device:TPU:0, one launch (start us, length us, event | category | flops | bytes accessed | tf_op | source)
XLA Modules:
  0.0 125.9 jit_solution(7966707215774378583)
XLA Ops:
  0.6 0.7 add_convert_fusion
  1.3 0.1 convert_element_type.11
  1.4 9.0 %gather.1.x_ref = bf16[48,576]{1,0:T(8,128)(2,1)} custom-call(s32[3,64]{1,0:T(4,128)} %tok_ref.1, bf16[576,122753]{1,0:T(8,128)(2,1)} %bitcast.edge_ref.emb_ref, bf16[576,122753]{1,0:T(8,128)(2,1)} %bitcast.edge_ref.emb_ref), custom_call_target="tpu_custom_call" | custom-call | tf_op jit(solution)/shard_map/gather/pallas_call | solution.py:64
  10.4 1.1 multiply_sine_fusion
  11.5 27.6 %qkv_sums.1.kvq_ref = bf16[3,192,576]{2,1,0:T(8,128)(2,1)} custom-call(bf16[48,576]{1,0:T(8,128)(2,1)} %gather.1.x_ref, bf16[576]{0:T(1024)(128)(2,1)} %g_ref.2, bf16[576,576]{1,0:T(8,128)(2,1)} %wk_hbm.1, bf16[576,576]{1,0:T(8,128)(2,1)} %wv_hbm.1, bf16[576,576]{1,0:T(8,128)(2,1)} %wq_hbm.1), custom_call_target="tpu_custom_call" | custom-call | flops 382205952 | bytes 2654208 | tf_op jit(solution)/shard_map/qkv_sums/pallas_call | solution.py:270
  39.2 19.1 %attention.1 = (bf16[192,576]{1,0:T(8,128)(2,1)}, bf16[64,9,64,128]{3,2,1,0:T(8,128)(2,1)}, bf16[64,9,64,128]{3,2,1,0:T(8,128)(2,1)}) custom-call(s32[64]{0:T(128)} %lens_ref.1, bf16[3,192,576]{2,1,0:T(8,128)(2,1)} %qkv_sums.1.kvq_ref, f32[192,32]{1,0:T(8,128)} %get-tuple-element.10.cos_ref, f32[192,32]{1,0:T(8,128)} %get-tuple-element.9.sin_ref, ...), custom_call_target="tpu_custom_call" | custom-call | flops 4000000000 | bytes 37748736 | tf_op jit(solution)/shard_map/attention/pallas_call | solution.py:154
  58.2 66.0 %moe.1 = bf16[192,576]{1,0:T(8,128)(2,1)} custom-call(bf16[192,576]{1,0:T(8,128)(2,1)} %get-tuple-element.6.o_ref, bf16[576,576]{1,0:T(8,128)(2,1)} %wo_hbm.1, bf16[48,576]{1,0:T(8,128)(2,1)} %gather.1.x_ref, bf16[576]{0:T(1024)(128)(2,1)} %g_ref.3, bf16[8,576]{1,0:T(8,128)(2,1)} %bitcast.15, s32[3,2,64]{2,1,0:T(2,128)} %bitcast.16, ...), custom_call_target="tpu_custom_call" | custom-call | flops 20000000000 | bytes 39813120 | tf_op jit(solution)/shard_map/moe/pallas_call | solution.py:463
  124.2 1.7 %copy.21 = bf16[3,64,576]{2,1,0:T(8,128)(2,1)} copy(bf16[3,64,576]{2,1,0:T(8,128)(2,1)} %bitcast.11) | data formatting | bytes 442368
  (1 shorter events, 0.0 us)
